TPU v7x, 1024 devices: a whole 4x8x16 slice. The times are simulated.
1024 devices in a mesh: section: 8 (over x, core), row: 8 (over y), col: 16 (over z).
Axes of the slice: x: 4, y: 8, z: 16, core: 2. Of those that a mesh axis runs over, the one named last changes fastest.
Arguments:
- hidden: bfloat16 [4, 32, 4096], P(None, None, 'col'), may hold values from -6 to 6
- norm_gain: bfloat16 [8, 4096], P('section', 'col'), may hold values from 0.25 to 1.75
- w_qkv: bfloat16 [8, 4096, 6144], P('section', 'col', 'row'), may hold values from -0.09375 to 0.09375
- w_out: bfloat16 [8, 4096, 4096], P('section', 'row', 'col'), may hold values from -0.09375 to 0.09375
- cache_keys: bfloat16 [8, 4, 32, 128, 8, 128], P('section', None, 'col', None, 'row'), may hold values from -240 to 240, as said below
- cache_values: bfloat16 [8, 4, 32, 128, 8, 128], P('section', None, 'col', None, 'row'), may hold values from -6 to 6
- cache_lengths: int32 [4, 32], P(None, 'col'), may hold values from 1 to 127
Outputs:
- layer_outputs: bfloat16 [8, 4, 32, 4096], P('section', None, None, 'col')
Inputs may be any that keep to these rules, and one draw needn't show every extreme that they name: `cache_keys`: cached keys are of order one except that some sequences may carry much larger keys at a few positions.
All inputs are finite; a program needn't handle non-finite values.
Results may differ from a plain program's by a relative error of at most 0.04.
Values may be sent and summed in bfloat16 or wider, within the bound.
A program may use at most 32 MiB of HBM per device.

v0:
```python
import math

import jax
import jax.numpy as jnp
from jax import lax
from jax.sharding import PartitionSpec as P

D = 4096
HEADS = 32
KVH = 8


def cut_along(x, dim, peers):
    before, after = (x.shape[:dim], x.shape[dim + 1 :])
    return jnp.moveaxis(x.reshape(*before, peers, -1, *after), dim, 0)


def sent_and_summed(x, axis, dim):
    parts = cut_along(x, dim, lax.axis_size(axis))
    arrived = lax.all_to_all(parts, axis, split_axis=0, concat_axis=0, tiled=True)
    return arrived.sum(axis=0)


def sent_together(arrays, axis, dim, along):
    widths = [math.prod(a.shape[along:]) for a in arrays]
    both = jnp.concatenate(
        [a.reshape(*a.shape[:along], w) for a, w in zip(arrays, widths)], axis=along
    )
    whole = sent_and_summed(both, axis, dim)
    parts = jnp.split(whole, [sum(widths[:k]) for k in range(1, len(widths))], axis=along)
    return tuple((b.reshape(*whole.shape[:along], *a.shape[along:]) for a, b in zip(arrays, parts)))


def laid_out(parts, dim):
    parts = jnp.moveaxis(parts, 0, dim)
    lengths = parts.shape
    return parts.reshape(*lengths[:dim], lengths[dim] * lengths[dim + 1], *lengths[dim + 2 :])


def sent_to_all(x, axis):
    copies = jnp.broadcast_to(x, (lax.axis_size(axis), *x.shape))
    return lax.all_to_all(copies, axis, split_axis=0, concat_axis=0, tiled=True)


def collect(x, axis, dim):
    return laid_out(sent_to_all(x, axis), dim)


def over_copies(x, axis):
    everything = sent_to_all(x, axis)
    return jnp.sum(everything, axis=0)


def from_behind(x, axis, by):
    peers = lax.axis_size(axis)
    pairs = [(i, i + by) for i in range(peers) if 0 <= i + by < peers]
    return lax.ppermute(x, axis, pairs)


def rotate(vectors, positions):
    half_dim = vectors.shape[-1] // 2
    inverse_freq = 500000.0 ** (-jnp.arange(half_dim, dtype=jnp.float32) * 2.0 / vectors.shape[-1])
    angles = positions * inverse_freq
    angles = jnp.concatenate([angles, angles], axis=-1)
    swapped = jnp.concatenate([-vectors[..., half_dim:], vectors[..., :half_dim]], axis=-1)
    return vectors * jnp.cos(angles) + swapped * jnp.sin(angles)


def attend(queries, new_key, new_value, key_block, value_block, length):
    score_scale = 1.0 / jnp.sqrt(jnp.float32(queries.shape[-1]))
    scores = (
        jnp.einsum("bgrd,bjgd->bgrj", queries, key_block, preferred_element_type=jnp.float32)
        * score_scale
    )
    own_score = (
        jnp.einsum("bgrd,bgd->bgr", queries, new_key, preferred_element_type=jnp.float32)
        * score_scale
    )
    visible = jnp.arange(key_block.shape[1])[None, :] < length[:, None]
    scores = jnp.where(visible[:, None, None, :], scores, -jnp.inf)
    row_max = jnp.maximum(jnp.max(scores, axis=-1), own_score)
    cache_exp = jnp.exp(scores - row_max[..., None])
    own_exp = jnp.exp(own_score - row_max)
    total = jnp.sum(cache_exp, axis=-1) + own_exp
    cache_weight = (cache_exp / total[..., None]).astype(jnp.bfloat16)
    own_weight = (own_exp / total).astype(jnp.bfloat16)
    result = jnp.einsum(
        "bgrj,bjgd->bgrd", cache_weight, value_block, preferred_element_type=jnp.float32
    )
    result = (
        result
        + own_weight.astype(jnp.float32)[..., None] * new_value.astype(jnp.float32)[:, :, None, :]
    )
    return result.astype(jnp.bfloat16)


def shards(hidden, norm_gain, w_qkv, w_out, cache_keys, cache_values, cache_lengths):
    section_count = lax.axis_size("section")
    section_at = lax.axis_index("section")
    col_count = lax.axis_size("col")
    micro_count = hidden.shape[0]
    batch_size = hidden.shape[1]
    seq_part = batch_size // col_count
    gain_row = norm_gain[0]
    proj_weight = w_qkv[0]
    out_weight = w_out[0]
    groups = cache_keys.shape[4]
    head_dim = cache_keys.shape[5]
    per_group = HEADS // KVH
    tick_count = micro_count + section_count - 1

    def layer_part(current, key_block, value_block, length):
        h_float = current.astype(jnp.float32)
        scaled = (h_float * gain_row.astype(jnp.float32)).astype(jnp.bfloat16)
        squares = jnp.sum(h_float * h_float, axis=1)
        partial_value = jnp.dot(scaled, proj_weight, preferred_element_type=jnp.float32)
        projected, own_squares = sent_together((partial_value, squares), "col", 0, 1)
        factor = lax.rsqrt(own_squares / D + 1e-05)
        projected = (projected * factor[:, None]).reshape(seq_part, groups, per_group + 2, head_dim)
        positions = length.astype(jnp.float32)
        queries = rotate(projected[:, :, :per_group], positions[:, None, None, None]).astype(
            jnp.bfloat16
        )
        new_key = rotate(projected[:, :, per_group], positions[:, None, None]).astype(jnp.bfloat16)
        new_value = projected[:, :, per_group + 1].astype(jnp.bfloat16)
        attended = attend(queries, new_key, new_value, key_block, value_block, length)
        attended = attended.reshape(seq_part, groups * per_group * head_dim)
        mixed_rows = jnp.dot(
            collect(attended, "col", 0), out_weight, preferred_element_type=jnp.float32
        )
        summed = over_copies(mixed_rows, "row")
        return (h_float + summed).astype(jnp.bfloat16)

    def advance(tick_at, loop_state):
        received, collected = loop_state
        micro_at = tick_at - section_at
        active = (micro_at >= 0) & (micro_at < micro_count)
        micro_pick = jnp.clip(micro_at, 0, micro_count - 1)
        entry_rows = lax.dynamic_index_in_dim(
            hidden, jnp.clip(tick_at, 0, micro_count - 1), 0, keepdims=False
        )
        current = jnp.where(section_at == 0, entry_rows, received)
        key_block = lax.dynamic_index_in_dim(cache_keys[0], micro_pick, 0, keepdims=False)
        value_block = lax.dynamic_index_in_dim(cache_values[0], micro_pick, 0, keepdims=False)
        length = lax.dynamic_index_in_dim(cache_lengths, micro_pick, 0, keepdims=False)
        produced = layer_part(current, key_block, value_block, length)
        previous = lax.dynamic_index_in_dim(collected, micro_pick, 0, keepdims=False)
        stored = jnp.where(active, produced, previous)
        collected = lax.dynamic_update_index_in_dim(collected, stored, micro_pick, 0)
        received = from_behind(produced, "section", 1)
        return (received, collected)

    start_rows = jnp.zeros(hidden.shape[1:], jnp.bfloat16)
    start_collected = jnp.zeros(hidden.shape, jnp.bfloat16)
    received, collected = lax.fori_loop(0, tick_count, advance, (start_rows, start_collected))
    return collected[None]


def solution(mesh):
    return jax.shard_map(
        shards,
        mesh=mesh,
        in_specs=(
            P(None, None, "col"),
            P("section", "col"),
            P("section", "col", "row"),
            P("section", "row", "col"),
            P("section", None, "col", None, "row", None),
            P("section", None, "col", None, "row", None),
            P(None, "col"),
        ),
        out_specs=P("section", None, None, "col"),
        check_vma=False,
    )
```

profile of v0, /device:TPU:7, one launch (start us, length us, event | category | flops | bytes accessed | tf_op | source)
XLA Modules:
  0.0 663.7 jit_solution(7477534044728916926)
XLA Ops:
  1.5 661.6 %while.18 = (s32[]{:T(128)}, bf16[32,256]{1,0:T(8,128)(2,1)S(1)}, bf16[4,32,256]{2,1,0:T(8,128)(2,1)S(1)}, pred[]{:T(512)}, bf16[4,32,256]{2,1,0:T(8,128)(2,1)},...) while((s32[]{:T(128)}, bf16[32,256]{1,0:T(8,128)(2,1)S(1)}, ...), condition=%wide.region_6.7_spmd, body=%wide.region_0.6_spmd.sunk | while | flops 21714148 | bytes 4714300 | solution.py:155
  4.4 18.6 %all-to-all-start = ((f32[16,2,769]{2,1,0:T(2,128)}), f32[16,2,769]{2,1,0:T(2,128)S(1)}, u32[]{:S(2)}, u32[]{:S(2)}) async-start(f32[16,2,769]{2,1,0:T(2,128)} %pad_maximum_fusion.3), calls=%async_computation | async-start | bytes 229376 | tf_op jit(solution)/shard_map/while/body/eval_jaxpr/all_to_all | solution.py:20
  23.2 11.7 %all-to-all-done = f32[16,2,769]{2,1,0:T(2,128)S(1)} async-done(((f32[16,2,769]{2,1,0:T(2,128)}), f32[16,2,769]{2,1,0:T(2,128)S(1)}, u32[]{:S(2)}, u32[]{:S(2)}) %all-to-all-start) | async-done | bytes 98464 | tf_op jit(solution)/shard_map/while/body/eval_jaxpr/all_to_all | solution.py:20
  38.0 16.8 %all_to_all.42 = bf16[16,2,512]{2,1,0:T(2,128)(2,1)S(1)} all-to-all(bf16[16,2,512]{2,1,0:T(2,128)(2,1)S(1)} %broadcast_in_dim.109), channel_id=1, replica_groups=mesh['section'=8,'row'=8,'col'=16] {'col'}, dimensions={0} | all-to-all | bytes 65536 | tf_op jit(solution)/shard_map/while/body/eval_jaxpr/all_to_all | solution.py:42
  62.5 9.4 %all-to-all-done.2 = f32[8,32,256]{2,1,0:T(8,128)S(1)} async-done(((f32[8,32,256]{2,1,0:T(8,128)}), f32[8,32,256]{2,1,0:T(8,128)S(1)}, u32[]{:S(2)}, u32[]{:S(2)}) %all-to-all-start.2) | async-done | bytes 262176 | tf_op jit(solution)/shard_map/while/body/eval_jaxpr/all_to_all | solution.py:42
  85.0 11.7 %all-to-all-done = f32[16,2,769]{2,1,0:T(2,128)S(1)} async-done(((f32[16,2,769]{2,1,0:T(2,128)}), f32[16,2,769]{2,1,0:T(2,128)S(1)}, u32[]{:S(2)}, u32[]{:S(2)}) %all-to-all-start) | async-done | bytes 98464 | tf_op jit(solution)/shard_map/while/body/eval_jaxpr/all_to_all | solution.py:20
  99.8 15.0 %all_to_all.42 = bf16[16,2,512]{2,1,0:T(2,128)(2,1)S(1)} all-to-all(bf16[16,2,512]{2,1,0:T(2,128)(2,1)S(1)} %broadcast_in_dim.109), channel_id=1, replica_groups=mesh['section'=8,'row'=8,'col'=16] {'col'}, dimensions={0} | all-to-all | bytes 65536 | tf_op jit(solution)/shard_map/while/body/eval_jaxpr/all_to_all | solution.py:42
  143.5 11.7 %all-to-all-done = f32[16,2,769]{2,1,0:T(2,128)S(1)} async-done(((f32[16,2,769]{2,1,0:T(2,128)}), f32[16,2,769]{2,1,0:T(2,128)S(1)}, u32[]{:S(2)}, u32[]{:S(2)}) %all-to-all-start) | async-done | bytes 98464 | tf_op jit(solution)/shard_map/while/body/eval_jaxpr/all_to_all | solution.py:20
  158.3 15.0 %all_to_all.42 = bf16[16,2,512]{2,1,0:T(2,128)(2,1)S(1)} all-to-all(bf16[16,2,512]{2,1,0:T(2,128)(2,1)S(1)} %broadcast_in_dim.109), channel_id=1, replica_groups=mesh['section'=8,'row'=8,'col'=16] {'col'}, dimensions={0} | all-to-all | bytes 65536 | tf_op jit(solution)/shard_map/while/body/eval_jaxpr/all_to_all | solution.py:42
  177.6 9.3 %all-to-all-done.2 = f32[8,32,256]{2,1,0:T(8,128)S(1)} async-done(((f32[8,32,256]{2,1,0:T(8,128)}), f32[8,32,256]{2,1,0:T(8,128)S(1)}, u32[]{:S(2)}, u32[]{:S(2)}) %all-to-all-start.2) | async-done | bytes 262176 | tf_op jit(solution)/shard_map/while/body/eval_jaxpr/all_to_all | solution.py:42
  202.0 11.7 %all-to-all-done = f32[16,2,769]{2,1,0:T(2,128)S(1)} async-done(((f32[16,2,769]{2,1,0:T(2,128)}), f32[16,2,769]{2,1,0:T(2,128)S(1)}, u32[]{:S(2)}, u32[]{:S(2)}) %all-to-all-start) | async-done | bytes 98464 | tf_op jit(solution)/shard_map/while/body/eval_jaxpr/all_to_all | solution.py:20
  216.7 15.0 %all_to_all.42 = bf16[16,2,512]{2,1,0:T(2,128)(2,1)S(1)} all-to-all(bf16[16,2,512]{2,1,0:T(2,128)(2,1)S(1)} %broadcast_in_dim.109), channel_id=1, replica_groups=mesh['section'=8,'row'=8,'col'=16] {'col'}, dimensions={0} | all-to-all | bytes 65536 | tf_op jit(solution)/shard_map/while/body/eval_jaxpr/all_to_all | solution.py:42
  236.1 9.3 %all-to-all-done.2 = f32[8,32,256]{2,1,0:T(8,128)S(1)} async-done(((f32[8,32,256]{2,1,0:T(8,128)}), f32[8,32,256]{2,1,0:T(8,128)S(1)}, u32[]{:S(2)}, u32[]{:S(2)}) %all-to-all-start.2) | async-done | bytes 262176 | tf_op jit(solution)/shard_map/while/body/eval_jaxpr/all_to_all | solution.py:42
  260.4 11.7 %all-to-all-done = f32[16,2,769]{2,1,0:T(2,128)S(1)} async-done(((f32[16,2,769]{2,1,0:T(2,128)}), f32[16,2,769]{2,1,0:T(2,128)S(1)}, u32[]{:S(2)}, u32[]{:S(2)}) %all-to-all-start) | async-done | bytes 98464 | tf_op jit(solution)/shard_map/while/body/eval_jaxpr/all_to_all | solution.py:20
  275.2 15.0 %all_to_all.42 = bf16[16,2,512]{2,1,0:T(2,128)(2,1)S(1)} all-to-all(bf16[16,2,512]{2,1,0:T(2,128)(2,1)S(1)} %broadcast_in_dim.109), channel_id=1, replica_groups=mesh['section'=8,'row'=8,'col'=16] {'col'}, dimensions={0} | all-to-all | bytes 65536 | tf_op jit(solution)/shard_map/while/body/eval_jaxpr/all_to_all | solution.py:42
  294.6 9.3 %all-to-all-done.2 = f32[8,32,256]{2,1,0:T(8,128)S(1)} async-done(((f32[8,32,256]{2,1,0:T(8,128)}), f32[8,32,256]{2,1,0:T(8,128)S(1)}, u32[]{:S(2)}, u32[]{:S(2)}) %all-to-all-start.2) | async-done | bytes 262176 | tf_op jit(solution)/shard_map/while/body/eval_jaxpr/all_to_all | solution.py:42
  318.9 11.7 %all-to-all-done = f32[16,2,769]{2,1,0:T(2,128)S(1)} async-done(((f32[16,2,769]{2,1,0:T(2,128)}), f32[16,2,769]{2,1,0:T(2,128)S(1)}, u32[]{:S(2)}, u32[]{:S(2)}) %all-to-all-start) | async-done | bytes 98464 | tf_op jit(solution)/shard_map/while/body/eval_jaxpr/all_to_all | solution.py:20
  333.7 15.0 %all_to_all.42 = bf16[16,2,512]{2,1,0:T(2,128)(2,1)S(1)} all-to-all(bf16[16,2,512]{2,1,0:T(2,128)(2,1)S(1)} %broadcast_in_dim.109), channel_id=1, replica_groups=mesh['section'=8,'row'=8,'col'=16] {'col'}, dimensions={0} | all-to-all | bytes 65536 | tf_op jit(solution)/shard_map/while/body/eval_jaxpr/all_to_all | solution.py:42
  353.0 9.3 %all-to-all-done.2 = f32[8,32,256]{2,1,0:T(8,128)S(1)} async-done(((f32[8,32,256]{2,1,0:T(8,128)}), f32[8,32,256]{2,1,0:T(8,128)S(1)}, u32[]{:S(2)}, u32[]{:S(2)}) %all-to-all-start.2) | async-done | bytes 262176 | tf_op jit(solution)/shard_map/while/body/eval_jaxpr/all_to_all | solution.py:42
  377.4 11.7 %all-to-all-done = f32[16,2,769]{2,1,0:T(2,128)S(1)} async-done(((f32[16,2,769]{2,1,0:T(2,128)}), f32[16,2,769]{2,1,0:T(2,128)S(1)}, u32[]{:S(2)}, u32[]{:S(2)}) %all-to-all-start) | async-done | bytes 98464 | tf_op jit(solution)/shard_map/while/body/eval_jaxpr/all_to_all | solution.py:20
  392.1 15.0 %all_to_all.42 = bf16[16,2,512]{2,1,0:T(2,128)(2,1)S(1)} all-to-all(bf16[16,2,512]{2,1,0:T(2,128)(2,1)S(1)} %broadcast_in_dim.109), channel_id=1, replica_groups=mesh['section'=8,'row'=8,'col'=16] {'col'}, dimensions={0} | all-to-all | bytes 65536 | tf_op jit(solution)/shard_map/while/body/eval_jaxpr/all_to_all | solution.py:42
  411.5 9.3 %all-to-all-done.2 = f32[8,32,256]{2,1,0:T(8,128)S(1)} async-done(((f32[8,32,256]{2,1,0:T(8,128)}), f32[8,32,256]{2,1,0:T(8,128)S(1)}, u32[]{:S(2)}, u32[]{:S(2)}) %all-to-all-start.2) | async-done | bytes 262176 | tf_op jit(solution)/shard_map/while/body/eval_jaxpr/all_to_all | solution.py:42
  435.8 11.7 %all-to-all-done = f32[16,2,769]{2,1,0:T(2,128)S(1)} async-done(((f32[16,2,769]{2,1,0:T(2,128)}), f32[16,2,769]{2,1,0:T(2,128)S(1)}, u32[]{:S(2)}, u32[]{:S(2)}) %all-to-all-start) | async-done | bytes 98464 | tf_op jit(solution)/shard_map/while/body/eval_jaxpr/all_to_all | solution.py:20
  450.6 15.0 %all_to_all.42 = bf16[16,2,512]{2,1,0:T(2,128)(2,1)S(1)} all-to-all(bf16[16,2,512]{2,1,0:T(2,128)(2,1)S(1)} %broadcast_in_dim.109), channel_id=1, replica_groups=mesh['section'=8,'row'=8,'col'=16] {'col'}, dimensions={0} | all-to-all | bytes 65536 | tf_op jit(solution)/shard_map/while/body/eval_jaxpr/all_to_all | solution.py:42
  494.3 11.7 %all-to-all-done = f32[16,2,769]{2,1,0:T(2,128)S(1)} async-done(((f32[16,2,769]{2,1,0:T(2,128)}), f32[16,2,769]{2,1,0:T(2,128)S(1)}, u32[]{:S(2)}, u32[]{:S(2)}) %all-to-all-start) | async-done | bytes 98464 | tf_op jit(solution)/shard_map/while/body/eval_jaxpr/all_to_all | solution.py:20
  509.1 15.0 %all_to_all.42 = bf16[16,2,512]{2,1,0:T(2,128)(2,1)S(1)} all-to-all(bf16[16,2,512]{2,1,0:T(2,128)(2,1)S(1)} %broadcast_in_dim.109), channel_id=1, replica_groups=mesh['section'=8,'row'=8,'col'=16] {'col'}, dimensions={0} | all-to-all | bytes 65536 | tf_op jit(solution)/shard_map/while/body/eval_jaxpr/all_to_all | solution.py:42
  552.8 11.7 %all-to-all-done = f32[16,2,769]{2,1,0:T(2,128)S(1)} async-done(((f32[16,2,769]{2,1,0:T(2,128)}), f32[16,2,769]{2,1,0:T(2,128)S(1)}, u32[]{:S(2)}, u32[]{:S(2)}) %all-to-all-start) | async-done | bytes 98464 | tf_op jit(solution)/shard_map/while/body/eval_jaxpr/all_to_all | solution.py:20
  567.5 15.0 %all_to_all.42 = bf16[16,2,512]{2,1,0:T(2,128)(2,1)S(1)} all-to-all(bf16[16,2,512]{2,1,0:T(2,128)(2,1)S(1)} %broadcast_in_dim.109), channel_id=1, replica_groups=mesh['section'=8,'row'=8,'col'=16] {'col'}, dimensions={0} | all-to-all | bytes 65536 | tf_op jit(solution)/shard_map/while/body/eval_jaxpr/all_to_all | solution.py:42
  586.9 9.3 %all-to-all-done.2 = f32[8,32,256]{2,1,0:T(8,128)S(1)} async-done(((f32[8,32,256]{2,1,0:T(8,128)}), f32[8,32,256]{2,1,0:T(8,128)S(1)}, u32[]{:S(2)}, u32[]{:S(2)}) %all-to-all-start.2) | async-done | bytes 262176 | tf_op jit(solution)/shard_map/while/body/eval_jaxpr/all_to_all | solution.py:42
  611.2 11.7 %all-to-all-done = f32[16,2,769]{2,1,0:T(2,128)S(1)} async-done(((f32[16,2,769]{2,1,0:T(2,128)}), f32[16,2,769]{2,1,0:T(2,128)S(1)}, u32[]{:S(2)}, u32[]{:S(2)}) %all-to-all-start) | async-done | bytes 98464 | tf_op jit(solution)/shard_map/while/body/eval_jaxpr/all_to_all | solution.py:20
  626.0 15.0 %all_to_all.42 = bf16[16,2,512]{2,1,0:T(2,128)(2,1)S(1)} all-to-all(bf16[16,2,512]{2,1,0:T(2,128)(2,1)S(1)} %broadcast_in_dim.109), channel_id=1, replica_groups=mesh['section'=8,'row'=8,'col'=16] {'col'}, dimensions={0} | all-to-all | bytes 65536 | tf_op jit(solution)/shard_map/while/body/eval_jaxpr/all_to_all | solution.py:42
  645.4 9.3 %all-to-all-done.2 = f32[8,32,256]{2,1,0:T(8,128)S(1)} async-done(((f32[8,32,256]{2,1,0:T(8,128)}), f32[8,32,256]{2,1,0:T(8,128)S(1)}, u32[]{:S(2)}, u32[]{:S(2)}) %all-to-all-start.2) | async-done | bytes 262176 | tf_op jit(solution)/shard_map/while/body/eval_jaxpr/all_to_all | solution.py:42
  (452 shorter events, 273.7 us)
Async XLA Ops:
  4.4 30.5 %all-to-all-start = ((f32[16,2,769]{2,1,0:T(2,128)}), f32[16,2,769]{2,1,0:T(2,128)S(1)}, u32[]{:S(2)}, u32[]{:S(2)}) async-start(f32[16,2,769]{2,1,0:T(2,128)} %pad_maximum_fusion.3), calls=%async_computation | async-start | bytes 229376 | tf_op jit(solution)/shard_map/while/body/eval_jaxpr/all_to_all | solution.py:20
  55.7 16.2 %all-to-all-start.2 = ((f32[8,32,256]{2,1,0:T(8,128)}), f32[8,32,256]{2,1,0:T(8,128)S(1)}, u32[]{:S(2)}, u32[]{:S(2)}) async-start(f32[8,32,256]{2,1,0:T(8,128)} %broadcast_in_dim.110), calls=%async_computation.2 | async-start | bytes 524288 | tf_op jit(solution)/shard_map/while/body/eval_jaxpr/all_to_all | solution.py:42
  81.3 15.4 %all-to-all-start = ((f32[16,2,769]{2,1,0:T(2,128)}), f32[16,2,769]{2,1,0:T(2,128)S(1)}, u32[]{:S(2)}, u32[]{:S(2)}) async-start(f32[16,2,769]{2,1,0:T(2,128)} %pad_maximum_fusion.3), calls=%async_computation | async-start | bytes 229376 | tf_op jit(solution)/shard_map/while/body/eval_jaxpr/all_to_all | solution.py:20
  115.7 12.8 %all-to-all-start.2 = ((f32[8,32,256]{2,1,0:T(8,128)}), f32[8,32,256]{2,1,0:T(8,128)S(1)}, u32[]{:S(2)}, u32[]{:S(2)}) async-start(f32[8,32,256]{2,1,0:T(8,128)} %broadcast_in_dim.110), calls=%async_computation.2 | async-start | bytes 524288 | tf_op jit(solution)/shard_map/while/body/eval_jaxpr/all_to_all | solution.py:42
  128.5 8.4 %collective-permute-start = (bf16[32,256]{1,0:T(8,128)(2,1)S(1)}, bf16[32,256]{1,0:T(8,128)(2,1)S(1)}, u32[]{:S(2)}, u32[]{:S(2)}) collective-permute-start(bf16[32,256]{1,0:T(8,128)(2,1)S(1)} %get-tuple-element.500), channel_id=1, source_target_pairs={{0,128},{128,256},{256,384},{384,512},{512,640},{640,768},{768,896... | collective-permute-start | bytes 49160 | tf_op jit(solution)/shard_map/while/body/eval_jaxpr/ppermute | solution.py:57
  139.8 15.4 %all-to-all-start = ((f32[16,2,769]{2,1,0:T(2,128)}), f32[16,2,769]{2,1,0:T(2,128)S(1)}, u32[]{:S(2)}, u32[]{:S(2)}) async-start(f32[16,2,769]{2,1,0:T(2,128)} %pad_maximum_fusion.3), calls=%async_computation | async-start | bytes 229376 | tf_op jit(solution)/shard_map/while/body/eval_jaxpr/all_to_all | solution.py:20
  174.2 12.8 %all-to-all-start.2 = ((f32[8,32,256]{2,1,0:T(8,128)}), f32[8,32,256]{2,1,0:T(8,128)S(1)}, u32[]{:S(2)}, u32[]{:S(2)}) async-start(f32[8,32,256]{2,1,0:T(8,128)} %broadcast_in_dim.110), calls=%async_computation.2 | async-start | bytes 524288 | tf_op jit(solution)/shard_map/while/body/eval_jaxpr/all_to_all | solution.py:42
  187.0 8.4 %collective-permute-start = (bf16[32,256]{1,0:T(8,128)(2,1)S(1)}, bf16[32,256]{1,0:T(8,128)(2,1)S(1)}, u32[]{:S(2)}, u32[]{:S(2)}) collective-permute-start(bf16[32,256]{1,0:T(8,128)(2,1)S(1)} %get-tuple-element.500), channel_id=1, source_target_pairs={{0,128},{128,256},{256,384},{384,512},{512,640},{640,768},{768,896... | collective-permute-start | bytes 49160 | tf_op jit(solution)/shard_map/while/body/eval_jaxpr/ppermute | solution.py:57
  198.3 15.4 %all-to-all-start = ((f32[16,2,769]{2,1,0:T(2,128)}), f32[16,2,769]{2,1,0:T(2,128)S(1)}, u32[]{:S(2)}, u32[]{:S(2)}) async-start(f32[16,2,769]{2,1,0:T(2,128)} %pad_maximum_fusion.3), calls=%async_computation | async-start | bytes 229376 | tf_op jit(solution)/shard_map/while/body/eval_jaxpr/all_to_all | solution.py:20
  232.6 12.8 %all-to-all-start.2 = ((f32[8,32,256]{2,1,0:T(8,128)}), f32[8,32,256]{2,1,0:T(8,128)S(1)}, u32[]{:S(2)}, u32[]{:S(2)}) async-start(f32[8,32,256]{2,1,0:T(8,128)} %broadcast_in_dim.110), calls=%async_computation.2 | async-start | bytes 524288 | tf_op jit(solution)/shard_map/while/body/eval_jaxpr/all_to_all | solution.py:42
  245.4 8.4 %collective-permute-start = (bf16[32,256]{1,0:T(8,128)(2,1)S(1)}, bf16[32,256]{1,0:T(8,128)(2,1)S(1)}, u32[]{:S(2)}, u32[]{:S(2)}) collective-permute-start(bf16[32,256]{1,0:T(8,128)(2,1)S(1)} %get-tuple-element.500), channel_id=1, source_target_pairs={{0,128},{128,256},{256,384},{384,512},{512,640},{640,768},{768,896... | collective-permute-start | bytes 49160 | tf_op jit(solution)/shard_map/while/body/eval_jaxpr/ppermute | solution.py:57
  256.7 15.4 %all-to-all-start = ((f32[16,2,769]{2,1,0:T(2,128)}), f32[16,2,769]{2,1,0:T(2,128)S(1)}, u32[]{:S(2)}, u32[]{:S(2)}) async-start(f32[16,2,769]{2,1,0:T(2,128)} %pad_maximum_fusion.3), calls=%async_computation | async-start | bytes 229376 | tf_op jit(solution)/shard_map/while/body/eval_jaxpr/all_to_all | solution.py:20
  291.1 12.8 %all-to-all-start.2 = ((f32[8,32,256]{2,1,0:T(8,128)}), f32[8,32,256]{2,1,0:T(8,128)S(1)}, u32[]{:S(2)}, u32[]{:S(2)}) async-start(f32[8,32,256]{2,1,0:T(8,128)} %broadcast_in_dim.110), calls=%async_computation.2 | async-start | bytes 524288 | tf_op jit(solution)/shard_map/while/body/eval_jaxpr/all_to_all | solution.py:42
  303.9 8.4 %collective-permute-start = (bf16[32,256]{1,0:T(8,128)(2,1)S(1)}, bf16[32,256]{1,0:T(8,128)(2,1)S(1)}, u32[]{:S(2)}, u32[]{:S(2)}) collective-permute-start(bf16[32,256]{1,0:T(8,128)(2,1)S(1)} %get-tuple-element.500), channel_id=1, source_target_pairs={{0,128},{128,256},{256,384},{384,512},{512,640},{640,768},{768,896... | collective-permute-start | bytes 49160 | tf_op jit(solution)/shard_map/while/body/eval_jaxpr/ppermute | solution.py:57
  315.2 15.4 %all-to-all-start = ((f32[16,2,769]{2,1,0:T(2,128)}), f32[16,2,769]{2,1,0:T(2,128)S(1)}, u32[]{:S(2)}, u32[]{:S(2)}) async-start(f32[16,2,769]{2,1,0:T(2,128)} %pad_maximum_fusion.3), calls=%async_computation | async-start | bytes 229376 | tf_op jit(solution)/shard_map/while/body/eval_jaxpr/all_to_all | solution.py:20
  349.6 12.8 %all-to-all-start.2 = ((f32[8,32,256]{2,1,0:T(8,128)}), f32[8,32,256]{2,1,0:T(8,128)S(1)}, u32[]{:S(2)}, u32[]{:S(2)}) async-start(f32[8,32,256]{2,1,0:T(8,128)} %broadcast_in_dim.110), calls=%async_computation.2 | async-start | bytes 524288 | tf_op jit(solution)/shard_map/while/body/eval_jaxpr/all_to_all | solution.py:42
  362.4 8.4 %collective-permute-start = (bf16[32,256]{1,0:T(8,128)(2,1)S(1)}, bf16[32,256]{1,0:T(8,128)(2,1)S(1)}, u32[]{:S(2)}, u32[]{:S(2)}) collective-permute-start(bf16[32,256]{1,0:T(8,128)(2,1)S(1)} %get-tuple-element.500), channel_id=1, source_target_pairs={{0,128},{128,256},{256,384},{384,512},{512,640},{640,768},{768,896... | collective-permute-start | bytes 49160 | tf_op jit(solution)/shard_map/while/body/eval_jaxpr/ppermute | solution.py:57
  373.7 15.4 %all-to-all-start = ((f32[16,2,769]{2,1,0:T(2,128)}), f32[16,2,769]{2,1,0:T(2,128)S(1)}, u32[]{:S(2)}, u32[]{:S(2)}) async-start(f32[16,2,769]{2,1,0:T(2,128)} %pad_maximum_fusion.3), calls=%async_computation | async-start | bytes 229376 | tf_op jit(solution)/shard_map/while/body/eval_jaxpr/all_to_all | solution.py:20
  408.0 12.8 %all-to-all-start.2 = ((f32[8,32,256]{2,1,0:T(8,128)}), f32[8,32,256]{2,1,0:T(8,128)S(1)}, u32[]{:S(2)}, u32[]{:S(2)}) async-start(f32[8,32,256]{2,1,0:T(8,128)} %broadcast_in_dim.110), calls=%async_computation.2 | async-start | bytes 524288 | tf_op jit(solution)/shard_map/while/body/eval_jaxpr/all_to_all | solution.py:42
  420.9 8.4 %collective-permute-start = (bf16[32,256]{1,0:T(8,128)(2,1)S(1)}, bf16[32,256]{1,0:T(8,128)(2,1)S(1)}, u32[]{:S(2)}, u32[]{:S(2)}) collective-permute-start(bf16[32,256]{1,0:T(8,128)(2,1)S(1)} %get-tuple-element.500), channel_id=1, source_target_pairs={{0,128},{128,256},{256,384},{384,512},{512,640},{640,768},{768,896... | collective-permute-start | bytes 49160 | tf_op jit(solution)/shard_map/while/body/eval_jaxpr/ppermute | solution.py:57
  432.1 15.4 %all-to-all-start = ((f32[16,2,769]{2,1,0:T(2,128)}), f32[16,2,769]{2,1,0:T(2,128)S(1)}, u32[]{:S(2)}, u32[]{:S(2)}) async-start(f32[16,2,769]{2,1,0:T(2,128)} %pad_maximum_fusion.3), calls=%async_computation | async-start | bytes 229376 | tf_op jit(solution)/shard_map/while/body/eval_jaxpr/all_to_all | solution.py:20
  466.5 12.8 %all-to-all-start.2 = ((f32[8,32,256]{2,1,0:T(8,128)}), f32[8,32,256]{2,1,0:T(8,128)S(1)}, u32[]{:S(2)}, u32[]{:S(2)}) async-start(f32[8,32,256]{2,1,0:T(8,128)} %broadcast_in_dim.110), calls=%async_computation.2 | async-start | bytes 524288 | tf_op jit(solution)/shard_map/while/body/eval_jaxpr/all_to_all | solution.py:42
  479.3 8.4 %collective-permute-start = (bf16[32,256]{1,0:T(8,128)(2,1)S(1)}, bf16[32,256]{1,0:T(8,128)(2,1)S(1)}, u32[]{:S(2)}, u32[]{:S(2)}) collective-permute-start(bf16[32,256]{1,0:T(8,128)(2,1)S(1)} %get-tuple-element.500), channel_id=1, source_target_pairs={{0,128},{128,256},{256,384},{384,512},{512,640},{640,768},{768,896... | collective-permute-start | bytes 49160 | tf_op jit(solution)/shard_map/while/body/eval_jaxpr/ppermute | solution.py:57
  490.6 15.4 %all-to-all-start = ((f32[16,2,769]{2,1,0:T(2,128)}), f32[16,2,769]{2,1,0:T(2,128)S(1)}, u32[]{:S(2)}, u32[]{:S(2)}) async-start(f32[16,2,769]{2,1,0:T(2,128)} %pad_maximum_fusion.3), calls=%async_computation | async-start | bytes 229376 | tf_op jit(solution)/shard_map/while/body/eval_jaxpr/all_to_all | solution.py:20
  525.0 12.8 %all-to-all-start.2 = ((f32[8,32,256]{2,1,0:T(8,128)}), f32[8,32,256]{2,1,0:T(8,128)S(1)}, u32[]{:S(2)}, u32[]{:S(2)}) async-start(f32[8,32,256]{2,1,0:T(8,128)} %broadcast_in_dim.110), calls=%async_computation.2 | async-start | bytes 524288 | tf_op jit(solution)/shard_map/while/body/eval_jaxpr/all_to_all | solution.py:42
  537.8 8.4 %collective-permute-start = (bf16[32,256]{1,0:T(8,128)(2,1)S(1)}, bf16[32,256]{1,0:T(8,128)(2,1)S(1)}, u32[]{:S(2)}, u32[]{:S(2)}) collective-permute-start(bf16[32,256]{1,0:T(8,128)(2,1)S(1)} %get-tuple-element.500), channel_id=1, source_target_pairs={{0,128},{128,256},{256,384},{384,512},{512,640},{640,768},{768,896... | collective-permute-start | bytes 49160 | tf_op jit(solution)/shard_map/while/body/eval_jaxpr/ppermute | solution.py:57
  549.1 15.4 %all-to-all-start = ((f32[16,2,769]{2,1,0:T(2,128)}), f32[16,2,769]{2,1,0:T(2,128)S(1)}, u32[]{:S(2)}, u32[]{:S(2)}) async-start(f32[16,2,769]{2,1,0:T(2,128)} %pad_maximum_fusion.3), calls=%async_computation | async-start | bytes 229376 | tf_op jit(solution)/shard_map/while/body/eval_jaxpr/all_to_all | solution.py:20
  583.5 12.8 %all-to-all-start.2 = ((f32[8,32,256]{2,1,0:T(8,128)}), f32[8,32,256]{2,1,0:T(8,128)S(1)}, u32[]{:S(2)}, u32[]{:S(2)}) async-start(f32[8,32,256]{2,1,0:T(8,128)} %broadcast_in_dim.110), calls=%async_computation.2 | async-start | bytes 524288 | tf_op jit(solution)/shard_map/while/body/eval_jaxpr/all_to_all | solution.py:42
  596.3 8.4 %collective-permute-start = (bf16[32,256]{1,0:T(8,128)(2,1)S(1)}, bf16[32,256]{1,0:T(8,128)(2,1)S(1)}, u32[]{:S(2)}, u32[]{:S(2)}) collective-permute-start(bf16[32,256]{1,0:T(8,128)(2,1)S(1)} %get-tuple-element.500), channel_id=1, source_target_pairs={{0,128},{128,256},{256,384},{384,512},{512,640},{640,768},{768,896... | collective-permute-start | bytes 49160 | tf_op jit(solution)/shard_map/while/body/eval_jaxpr/ppermute | solution.py:57
  607.5 15.4 %all-to-all-start = ((f32[16,2,769]{2,1,0:T(2,128)}), f32[16,2,769]{2,1,0:T(2,128)S(1)}, u32[]{:S(2)}, u32[]{:S(2)}) async-start(f32[16,2,769]{2,1,0:T(2,128)} %pad_maximum_fusion.3), calls=%async_computation | async-start | bytes 229376 | tf_op jit(solution)/shard_map/while/body/eval_jaxpr/all_to_all | solution.py:20
  641.9 12.8 %all-to-all-start.2 = ((f32[8,32,256]{2,1,0:T(8,128)}), f32[8,32,256]{2,1,0:T(8,128)S(1)}, u32[]{:S(2)}, u32[]{:S(2)}) async-start(f32[8,32,256]{2,1,0:T(8,128)} %broadcast_in_dim.110), calls=%async_computation.2 | async-start | bytes 524288 | tf_op jit(solution)/shard_map/while/body/eval_jaxpr/all_to_all | solution.py:42
  654.7 8.4 %collective-permute-start = (bf16[32,256]{1,0:T(8,128)(2,1)S(1)}, bf16[32,256]{1,0:T(8,128)(2,1)S(1)}, u32[]{:S(2)}, u32[]{:S(2)}) collective-permute-start(bf16[32,256]{1,0:T(8,128)(2,1)S(1)} %get-tuple-element.500), channel_id=1, source_target_pairs={{0,128},{128,256},{256,384},{384,512},{512,640},{640,768},{768,896... | collective-permute-start | bytes 49160 | tf_op jit(solution)/shard_map/while/body/eval_jaxpr/ppermute | solution.py:57
  (15 other events, 205.7 us)
where the time goes:
time: 672 us; the launch traced here: 664 us
  waiting for transfers between devices  307 us (46%)
  blocking collectives  167 us (25%)
  starting transfers between devices  109 us (16%)
  matrix products  39.1 us (6%)
  other arithmetic  27.7 us (4%)
  local copies, waits for them, and re-layouts  12.8 us (2%)
    all_to_all x11, blocking collectives, sent_to_all(): return lax.all_to_all(copies, axis, split_axis=0, concat_axis=0, tiled=True)  167 us
    all_to_all x11, waiting for transfers between devices, sent_and_summed(): lax.all_to_all(parts, axis, split_axis=0, concat_axis=0, tiled=True)  128 us
    all_to_all x11, waiting for transfers between devices, sent_to_all(): return lax.all_to_all(copies, axis, split_axis=0, concat_axis=0, tiled=True)  103 us
    ppermute x11, waiting for transfers between devices, from_behind(): return lax.ppermute(x, axis, pairs)  76 us
    all_to_all x11, starting transfers between devices, sent_and_summed(): lax.all_to_all(parts, axis, split_axis=0, concat_axis=0, tiled=True)  53.7 us
    all_to_all x11, starting transfers between devices, sent_to_all(): return lax.all_to_all(copies, axis, split_axis=0, concat_axis=0, tiled=True)  40.9 us
    ppermute x11, starting transfers between devices, from_behind(): return lax.ppermute(x, axis, pairs)  14.2 us
  transfers between devices with their start and end apart: 33, of which 33 were waited for; matrix products, arithmetic and copies ran while one was open for 0% of the time, Pallas kernels for 0%

commit v1 on v0

v1 whole, which is shorter than its diff:
```python
import functools
import math

import jax
import jax.numpy as jnp
from jax import lax
from jax.experimental import pallas as pl
from jax.experimental.pallas import tpu as pltpu
from jax.sharding import PartitionSpec as P

D = 4096
HEADS = 32
KVH = 8
MESH = pl.DeviceIdType.MESH


def far_first(n):
    order = []
    for k in range(n // 2, 0, -1):
        order.append(k)
        if n - k != k:
            order.append(n - k)
    return order


def kernel(
    sizes,
    lens_ref,
    hidden_ref,
    gain_ref,
    wq_hbm,
    wo_hbm,
    keys_hbm,
    vals_hbm,
    out_ref,
    wq,
    wo,
    keys,
    vals,
    cos8,
    sin8,
    state,
    prev,
    pin,
    rs_out,
    rs_in,
    att,
    po,
    load_sem,
    rs_send,
    rs_recv,
    att_send,
    att_recv,
    po_send,
    po_recv,
    prev_send,
    prev_recv,
    out_send,
    out_recv,
):
    n_sec, n_row, n_col = sizes
    s = lax.axis_index("section")
    r = lax.axis_index("row")
    c = lax.axis_index("col")
    last = n_sec - 1
    micro, batch, feats = state.shape
    seqs = batch // n_col
    hd = keys.shape[-1]
    length = keys.shape[2]
    width = wq.shape[1]
    per_group = HEADS // KVH
    rows8 = per_group * seqs

    def at(sec, row, col):
        return {"section": sec, "row": row, "col": col}

    loads = [
        pltpu.make_async_copy(wq_hbm, wq, load_sem.at[0]),
        pltpu.make_async_copy(wo_hbm, wo, load_sem.at[1]),
        pltpu.make_async_copy(keys_hbm, keys, load_sem.at[2]),
        pltpu.make_async_copy(vals_hbm, vals, load_sem.at[3]),
    ]
    for load in loads:
        load.start()

    barrier = pltpu.get_barrier_semaphore()

    def greet(device):
        pl.semaphore_signal(barrier, inc=1, device_id=device, device_id_type=MESH)

    for j in far_first(n_col):
        greet(at(s, r, lax.rem(c + j, n_col)))

    @pl.when(s < last)
    def _():
        for j in range(n_row):
            greet(at(s + 1, lax.rem(r + j, n_row), c))

    @pl.when(s > 0)
    def _():
        for j in range(n_row):
            greet(at(s - 1, lax.rem(r + j, n_row), c))

    @pl.when(s == last)
    def _():
        for j in range(1, n_row):
            greet(at(s, lax.rem(r + j, n_row), c))

    lane = lax.broadcasted_iota(jnp.int32, (rows8, hd), 1)
    row8 = lax.broadcasted_iota(jnp.int32, (rows8, hd), 0)
    half = lax.rem(lane, hd // 2).astype(jnp.float32)
    inverse_freq = jnp.exp(half * (-2.0 / hd * math.log(500000.0)))
    sign = jnp.where(lane < hd // 2, -1.0, 1.0)

    def lengths_of(m):
        value = jnp.full((rows8, hd), lens_ref[m * seqs], jnp.int32)
        for b in range(1, seqs):
            value = jnp.where(lax.rem(row8, seqs) == b, lens_ref[m * seqs + b], value)
        return value

    for m in range(micro):
        angle = lengths_of(m).astype(jnp.float32) * inverse_freq
        cos8[m] = jnp.cos(angle)
        sin8[m] = jnp.sin(angle) * sign

    loads[0].wait()
    pl.semaphore_wait(
        barrier,
        n_col
        - 1
        + jnp.where(s < last, n_row, 0)
        + jnp.where(s > 0, n_row, 0)
        + jnp.where(s == last, n_row - 1, 0),
    )

    def summed(region, m, base):
        total = pin[region, m, 0].astype(jnp.float32)
        for k in range(1, n_row):
            total = total + pin[region, m, k].astype(jnp.float32)
        return (base.astype(jnp.float32) + total).astype(jnp.bfloat16)

    gain = gain_ref[...].astype(jnp.float32)

    def stage_a(m, carry):
        @pl.when(s == 0)
        def _():
            state[m] = hidden_ref[m]

        @pl.when(s > 0)
        def _():
            pltpu.make_async_copy(prev.at[m], prev.at[m], prev_recv.at[m]).wait()
            pltpu.make_async_copy(pin.at[0, m], pin.at[0, m], po_recv.at[0, m]).wait()
            state[m] = summed(0, m, prev[m])

        h_float = state[m].astype(jnp.float32)
        scaled = (h_float * gain).astype(jnp.bfloat16)
        partial = jnp.dot(scaled, wq[...], preferred_element_type=jnp.float32)
        squares = jnp.sum(h_float * h_float, axis=1, keepdims=True)
        squares = jnp.broadcast_to(squares, (batch, hd))
        for k in range(n_col):
            rs_out[m, k, :, 0:width] = partial[k * seqs : (k + 1) * seqs]
            rs_out[m, k, :, width : width + hd] = squares[k * seqs : (k + 1) * seqs]
        for j in far_first(n_col):
            to = lax.rem(c + j, n_col)
            pltpu.make_async_remote_copy(
                src_ref=rs_out.at[m, to],
                dst_ref=rs_in.at[m, j - 1],
                send_sem=rs_send.at[m],
                recv_sem=rs_recv.at[m],
                device_id=at(s, r, to),
                device_id_type=MESH,
            ).start()

        @pl.when(s < last)
        def _():
            pltpu.make_async_remote_copy(
                src_ref=state.at[m],
                dst_ref=prev.at[m],
                send_sem=prev_send.at[m],
                recv_sem=prev_recv.at[m],
                device_id=at(s + 1, r, c),
                device_id_type=MESH,
            ).start()

        @pl.when(s > 0)
        def _():
            pltpu.make_async_remote_copy(
                src_ref=state.at[m],
                dst_ref=out_ref.at[m],
                send_sem=out_send.at[m],
                recv_sem=out_recv.at[m],
                device_id=at(s - 1, r, c),
                device_id_type=MESH,
            ).start()

        return carry

    lax.fori_loop(0, micro, stage_a, 0)

    loads[2].wait()
    loads[3].wait()
    score_scale = 1.0 / math.sqrt(hd)

    def stage_b(m, carry):
        pltpu.make_async_copy(rs_in.at[m], rs_in.at[m], rs_recv.at[m]).wait()
        total = rs_out[m, c]
        for j in range(n_col - 1):
            total = total + rs_in[m, j]
        factor = lax.rsqrt(total[:, width : width + hd] / D + 1e-05)
        heads = [total[:, h * hd : (h + 1) * hd] * factor for h in range(per_group + 2)]
        cos = cos8[m]
        sin = sin8[m]

        def rotate(x):
            return (x * cos + pltpu.roll(x, hd // 2, 1) * sin).astype(jnp.bfloat16)

        queries = rotate(jnp.concatenate(heads[:per_group], axis=0))
        new_key = rotate(jnp.concatenate([heads[per_group]] * per_group, axis=0))
        new_value = jnp.concatenate([heads[per_group + 1]] * per_group, axis=0)
        new_value = new_value.astype(jnp.bfloat16).astype(jnp.float32)
        which = lax.rem(row8, seqs)
        scores = None
        for b in range(seqs):
            mine = lax.dot_general(
                queries,
                keys[m, b],
                (((1,), (1,)), ((), ())),
                preferred_element_type=jnp.float32,
            )
            scores = mine if b == 0 else jnp.where(which == b, mine, scores)
        scores = scores * score_scale
        own = queries.astype(jnp.float32) * new_key.astype(jnp.float32)
        own = jnp.sum(own, axis=1, keepdims=True) * score_scale
        scores = jnp.where(lane < lengths_of(m), scores, -jnp.inf)
        top = jnp.maximum(jnp.max(scores, axis=1, keepdims=True), own)
        cache_exp = jnp.exp(scores - top)
        own_exp = jnp.exp(own - top)
        denom = jnp.sum(cache_exp, axis=1, keepdims=True) + own_exp
        weight = (cache_exp / denom).astype(jnp.bfloat16)
        own_weight = (own_exp / denom).astype(jnp.bfloat16).astype(jnp.float32)
        result = None
        for b in range(seqs):
            mine = jnp.dot(weight, vals[m, b], preferred_element_type=jnp.float32)
            result = mine if b == 0 else jnp.where(which == b, mine, result)
        result = (result + own_weight * new_value).astype(jnp.bfloat16)
        for h in range(per_group):
            att[m, c, :, h * hd : (h + 1) * hd] = result[h * seqs : (h + 1) * seqs]
        for j in far_first(n_col):
            pltpu.make_async_remote_copy(
                src_ref=att.at[m, c],
                dst_ref=att.at[m, c],
                send_sem=att_send.at[m],
                recv_sem=att_recv.at[m],
                device_id=at(s, r, lax.rem(c + j, n_col)),
                device_id_type=MESH,
            ).start()
        return carry

    lax.fori_loop(0, micro, stage_b, 0)

    loads[1].wait()
    region = jnp.where(s == last, 1, 0)
    target = jnp.where(s == last, last, s + 1)

    def stage_c(m, carry):
        others = att.at[m, pl.ds(0, n_col - 1)]
        pltpu.make_async_copy(others, others, att_recv.at[m]).wait()
        rows = jnp.concatenate([att[m, k] for k in range(n_col)], axis=0)
        mixed = jnp.dot(rows, wo[...], preferred_element_type=jnp.float32).astype(jnp.bfloat16)
        po[m] = mixed

        @pl.when(s == last)
        def _():
            pin[1, m, r] = mixed

        def send(j):
            pltpu.make_async_remote_copy(
                src_ref=po.at[m],
                dst_ref=pin.at[region, m, r],
                send_sem=po_send.at[m],
                recv_sem=po_recv.at[region, m],
                device_id=at(target, lax.rem(r + j, n_row), c),
                device_id_type=MESH,
            ).start()

        for j in far_first(n_row):
            send(j)

        @pl.when(s < last)
        def _():
            send(0)

        return carry

    lax.fori_loop(0, micro, stage_c, 0)

    def finish(m, carry):
        @pl.when(s == last)
        def _():
            others = pin.at[1, m, pl.ds(0, n_row - 1)]
            pltpu.make_async_copy(others, others, po_recv.at[1, m]).wait()
            out_ref[m] = summed(1, m, state[m])
            pltpu.make_async_copy(others, others, po_send.at[m]).wait()

        @pl.when(s < last)
        def _():
            pltpu.make_async_copy(out_ref.at[m], out_ref.at[m], out_recv.at[m]).wait()
            pltpu.make_async_copy(state.at[m], state.at[m], prev_send.at[m]).wait()
            pltpu.make_async_copy(pin.at[0, m], pin.at[0, m], po_send.at[m]).wait()

        @pl.when(s > 0)
        def _():
            pltpu.make_async_copy(state.at[m], state.at[m], out_send.at[m]).wait()

        pltpu.make_async_copy(rs_in.at[m], rs_in.at[m], rs_send.at[m]).wait()
        others = att.at[m, pl.ds(0, n_col - 1)]
        pltpu.make_async_copy(others, others, att_send.at[m]).wait()
        return carry

    lax.fori_loop(0, micro, finish, 0)


def solution(mesh):
    n_sec, n_row, n_col = mesh.shape["section"], mesh.shape["row"], mesh.shape["col"]

    def shards(hidden, norm_gain, w_qkv, w_out, cache_keys, cache_values, cache_lengths):
        micro, batch, feats = hidden.shape
        wq = w_qkv[0]
        wo = w_out[0]
        width = wq.shape[1]
        _, _, seqs, length, groups, hd = cache_keys.shape
        keys = cache_keys.reshape(micro, seqs, length, hd)
        vals = cache_values.reshape(micro, seqs, length, hd)
        rows8 = HEADS // KVH * seqs
        bf, f32 = jnp.bfloat16, jnp.float32
        vmem = pl.BlockSpec(memory_space=pltpu.VMEM)
        hbm = pl.BlockSpec(memory_space=pl.ANY)
        sem = pltpu.SemaphoreType.DMA
        out = pl.pallas_call(
            functools.partial(kernel, (n_sec, n_row, n_col)),
            out_shape=jax.ShapeDtypeStruct((micro, batch, feats), bf),
            in_specs=[pl.BlockSpec(memory_space=pltpu.SMEM), vmem, vmem, hbm, hbm, hbm, hbm],
            out_specs=vmem,
            scratch_shapes=[
                pltpu.VMEM(wq.shape, bf),
                pltpu.VMEM(wo.shape, bf),
                pltpu.VMEM(keys.shape, bf),
                pltpu.VMEM(vals.shape, bf),
                pltpu.VMEM((micro, rows8, hd), f32),
                pltpu.VMEM((micro, rows8, hd), f32),
                pltpu.VMEM((micro, batch, feats), bf),
                pltpu.VMEM((micro, batch, feats), bf),
                pltpu.VMEM((2, micro, n_row, batch, feats), bf),
                pltpu.VMEM((micro, n_col, seqs, width + hd), f32),
                pltpu.VMEM((micro, n_col - 1, seqs, width + hd), f32),
                pltpu.VMEM((micro, n_col, seqs, wo.shape[0]), bf),
                pltpu.VMEM((micro, batch, feats), bf),
                sem((4,)),
                sem((micro,)),
                sem((micro,)),
                sem((micro,)),
                sem((micro,)),
                sem((micro,)),
                sem((2, micro)),
                sem((micro,)),
                sem((micro,)),
                sem((micro,)),
                sem((micro,)),
            ],
            compiler_params=pltpu.CompilerParams(collective_id=0, has_side_effects=True),
        )(cache_lengths.reshape(-1), hidden, norm_gain, wq, wo, keys, vals)
        return out[None]

    return jax.shard_map(
        shards,
        mesh=mesh,
        in_specs=(
            P(None, None, "col"),
            P("section", "col"),
            P("section", "col", "row"),
            P("section", "row", "col"),
            P("section", None, "col", None, "row", None),
            P("section", None, "col", None, "row", None),
            P(None, "col"),
        ),
        out_specs=P("section", None, None, "col"),
        check_vma=False,
    )
```

time: 672 us -> 205 us (0.31); the launches traced: 664 us -> 205 us
  waiting for transfers between devices: 307 us -> 0 us
  Pallas kernels: 0 us -> 202 us
  blocking collectives: 167 us -> 0 us
  starting transfers between devices: 109 us -> 0 us
  matrix products: 39.1 us -> 0 us
  other arithmetic: 27.7 us -> 0 us
  local copies, waits for them, and re-layouts: 12.8 us -> 2.84 us
    all_to_all x22 -> x0, waiting for transfers between devices: 231 us -> none  [the longest x11 128 us: sent_and_summed(): lax.all_to_all(parts, axis, split_axis=0, concat_axis=0, tiled=True)]
    pallas_call x0 -> x1, Pallas kernels: none -> 202 us  [shards(): pl.pallas_call(functools.partial(kernel, (n_sec, n_row, n_col)), out_shap...]
    all_to_all x11 -> x0, blocking collectives: 167 us -> none  [sent_to_all(): return lax.all_to_all(copies, axis, split_axis=0, concat_axis=0, tiled=True)]
    all_to_all x22 -> x0, starting transfers between devices: 94.6 us -> none  [the longest x11 53.7 us: sent_and_summed(): lax.all_to_all(parts, axis, split_axis=0, concat_axis=0, tiled=True)]
    ppermute x11 -> x0, waiting for transfers between devices: 76 us -> none  [from_behind(): return lax.ppermute(x, axis, pairs)]
    dot_general x55 -> x0, matrix products: 39.1 us -> none  [the longest x11 13.1 us: layer_part(): jnp.dot(scaled, proj_weight, preferred_element_type=jnp.float32)]
    ppermute x11 -> x0, starting transfers between devices: 14.2 us -> none  [from_behind(): return lax.ppermute(x, axis, pairs)]
    reduce_sum x44 -> x0, other arithmetic: 11.8 us -> none  [the longest x11 9.15 us: layer_part(): squares = jnp.sum(h_float * h_float, axis=1)]
  transfers between devices with their start and end apart: 33 -> 0, of which waited for: 33 -> 0; matrix products, arithmetic and copies ran while one was open for 0% -> 0% of each run, Pallas kernels for 0% -> 0%
where the time goes in v1:
time: 205 us
  Pallas kernels  202 us (99%)
  local copies, waits for them, and re-layouts  2.84 us (1%)
    pallas_call x1, Pallas kernels, shards(): pl.pallas_call(functools.partial(kernel, (n_sec, n_row, n_col)), out_shap...  202 us

profile of v1, /device:TPU:7, one launch (start us, length us, event | category | flops | bytes accessed | tf_op | source)
XLA Modules:
  0.0 204.8 jit_solution(11926941746481942835)
XLA Ops:
  0.0 0.0 copy-start
  0.0 0.7 copy-done
  0.7 0.1 copy.9
  0.8 0.6 reshape.9.lens_ref
  1.4 201.9 %shard_map.73 = bf16[4,32,256]{2,1,0:T(8,128)(2,1)} custom-call(s32[8]{0:T(128)} %reshape.9.lens_ref, bf16[4,32,256]{2,1,0:T(8,128)(2,1)} %hidden_ref.1, bf16[1,256]{1,0:T(2,128)(2,1)} %gain_ref.1, bf16[256,768]{1,0:T(8,128)(2,1)} %bitcast.5, bf16[512,256]{1,0:T(8,128)(2,1)} %bitcast.7, bf16[4,2,128,128]{3,2,1,0:T(8,128)(2,1)} %bitcast.8, ...), custom_call_target="tpu_custom_call" | custom-call | tf_op jit(solution)/shard_map/pallas_call | solution.py:339
  203.3 1.5 copy.11
Async XLA Ops:
  0.0 0.7 copy-start

commit v2 on v1

v2 whole, which is shorter than its diff:
```python
import functools
import math

import jax
import jax.numpy as jnp
from jax import lax
from jax.experimental import pallas as pl
from jax.experimental.pallas import tpu as pltpu
from jax.sharding import PartitionSpec as P

D = 4096
HEADS = 32
KVH = 8
MESH = pl.DeviceIdType.MESH
BY_SEQUENCE = (1, 3, 4, 6)
CHUNKS = 4


def far_first(n):
    order = []
    for k in range(n // 2, 0, -1):
        order.append(k)
        if n - k != k:
            order.append(n - k)
    return order


def one_of(value, choices):
    hit = value < 0
    for choice in choices:
        hit = hit | (value == choice)
    return hit


def rows_of(ref, index, count):
    return jnp.concatenate([ref[index, k] for k in range(count)], axis=0)


def kernel(
    sizes,
    lens_ref,
    hidden_ref,
    gain_ref,
    wq_hbm,
    wo_hbm,
    keys_hbm,
    vals_hbm,
    out_ref,
    wq,
    wo,
    keys,
    vals,
    cos8,
    sin8,
    gains,
    gain32,
    rows,
    state,
    prev,
    given,
    pin,
    rs_out,
    rs_in,
    total,
    att,
    po,
    load_sem,
    wq_send,
    wq_recv,
    wo_send,
    wo_recv,
    gain_send,
    gain_recv,
    go_sem,
    rs_send,
    rs_recv,
    att_send,
    att_recv,
    po_send,
    po_recv,
    prev_send,
    prev_recv,
    out_send,
    out_recv,
):
    n_sec, n_row, n_col = sizes
    s = lax.axis_index("section")
    r = lax.axis_index("row")
    c = lax.axis_index("col")
    last = n_sec - 1
    micro, n_blocks, seqs, feats = state.shape
    batch = n_col * seqs
    hd = keys.shape[-1]
    width = wq.shape[1]
    per_group = HEADS // KVH
    rows8 = per_group * seqs
    out_seq = one_of(s, BY_SEQUENCE)
    out_feat = jnp.logical_not(out_seq)
    in_seq = one_of(s, [b + 1 for b in BY_SEQUENCE])
    in_feat = jnp.logical_not(in_seq)
    right, left = lax.rem(c + 1, n_col), lax.rem(c + n_col - 1, n_col)

    def at(sec, row, col):
        return {"section": sec, "row": row, "col": col}

    my_rows = pl.ds(pl.multiple_of(c * feats, feats), feats)
    load_wq = pltpu.make_async_copy(wq_hbm, wq.at[my_rows], load_sem.at[0])
    load_wo = pltpu.make_async_copy(wo_hbm, wo.at[c], load_sem.at[1])
    load_keys = pltpu.make_async_copy(keys_hbm, keys, load_sem.at[2])
    load_vals = pltpu.make_async_copy(vals_hbm, vals, load_sem.at[3])
    load_wq.start()
    load_wo.start()
    load_keys.start()
    load_vals.start()

    barrier = pltpu.get_barrier_semaphore()

    def greet(device):
        pl.semaphore_signal(barrier, inc=1, device_id=device, device_id_type=MESH)

    for j in far_first(n_col):
        greet(at(s, r, lax.rem(c + j, n_col)))

    @pl.when(s < last)
    def _():
        for j in range(n_row):
            greet(at(s + 1, lax.rem(r + j, n_row), c))
        for j in range(1, n_col):
            greet(at(s + 1, r, lax.rem(c + j, n_col)))

    @pl.when(s > 0)
    def _():
        for j in range(n_row):
            greet(at(s - 1, lax.rem(r + j, n_row), c))
        for j in range(1, n_col):
            greet(at(s - 1, r, lax.rem(c + j, n_col)))

    @pl.when(s == last)
    def _():
        for j in range(1, n_row):
            greet(at(s, lax.rem(r + j, n_row), c))

    lane = lax.broadcasted_iota(jnp.int32, (rows8, hd), 1)
    row8 = lax.broadcasted_iota(jnp.int32, (rows8, hd), 0)
    half = lax.rem(lane, hd // 2).astype(jnp.float32)
    inverse_freq = jnp.exp(half * (-2.0 / hd * math.log(500000.0)))
    sign = jnp.where(lane < hd // 2, -1.0, 1.0)

    def lengths_of(m):
        value = jnp.full((rows8, hd), lens_ref[m * seqs], jnp.int32)
        for b in range(1, seqs):
            value = jnp.where(lax.rem(row8, seqs) == b, lens_ref[m * seqs + b], value)
        return value

    for m in range(micro):
        angle = lengths_of(m).astype(jnp.float32) * inverse_freq
        cos8[m] = jnp.cos(angle)
        sin8[m] = jnp.sin(angle) * sign
    gain32[...] = jnp.broadcast_to(gain_ref[...].astype(jnp.float32), gain32.shape)
    gains[c] = gain_ref[...]

    load_wq.wait()
    load_wo.wait()
    across = n_row + n_col - 1
    pl.semaphore_wait(
        barrier,
        n_col
        - 1
        + jnp.where(s < last, across, 0)
        + jnp.where(s > 0, across, 0)
        + jnp.where(s == last, n_row - 1, 0),
    )

    def gather(part, send_sem, recv_sem):
        def copy(way, step, block, piece, to):
            return pltpu.make_async_remote_copy(
                src_ref=part(block, piece),
                dst_ref=part(block, piece),
                send_sem=send_sem,
                recv_sem=recv_sem.at[way, step, piece],
                device_id=at(s, r, to),
                device_id_type=MESH,
            )

        def arrived(way, step, piece):
            pltpu.make_async_copy(part(0, 0), part(0, 0), recv_sem.at[way, step, piece]).wait()

        for piece in range(CHUNKS):
            copy(0, 0, c, piece, right).start()
            copy(1, 0, c, piece, left).start()

        rightward, leftward = n_col // 2, n_col - 1 - n_col // 2

        def forward(step, carry):
            for piece in range(CHUNKS):
                arrived(0, step - 1, piece)
                copy(0, step, lax.rem(c + n_col - step, n_col), piece, right).start()

                @pl.when(step < leftward)
                def _():
                    arrived(1, step - 1, piece)
                    copy(1, step, lax.rem(c + step, n_col), piece, left).start()

            return carry

        lax.fori_loop(1, rightward, forward, 0)
        for piece in range(CHUNKS):
            arrived(0, rightward - 1, piece)
            arrived(1, leftward - 1, piece)

        def sent(k, carry):
            for piece in range(CHUNKS):
                pltpu.make_async_copy(part(0, 0), part(0, 0), send_sem).wait()
            return carry

        lax.fori_loop(0, n_col - 1, sent, 0)

    piece_rows = feats // CHUNKS

    def wq_part(block, piece):
        first = pl.multiple_of(block * feats + piece * piece_rows, piece_rows)
        return wq.at[pl.ds(first, piece_rows)]

    wo_rows = wo.shape[1] // CHUNKS

    def wo_part(block, piece):
        return wo.at[block, pl.ds(piece * wo_rows, wo_rows)]

    odd = lax.rem(s, 2) == 1

    @pl.when(odd & (s > 1))
    def _():
        pl.semaphore_wait(go_sem, 1)

    @pl.when(in_seq)
    def _():
        for j in far_first(n_col):
            pltpu.make_async_remote_copy(
                src_ref=gains.at[c],
                dst_ref=gains.at[c],
                send_sem=gain_send,
                recv_sem=gain_recv,
                device_id=at(s, r, lax.rem(c + j, n_col)),
                device_id_type=MESH,
            ).start()
        gather(wq_part, wq_send, wq_recv)
        others = gains.at[pl.ds(0, n_col - 1)]
        pltpu.make_async_copy(others, others, gain_recv).wait()
        pltpu.make_async_copy(others, others, gain_send).wait()
        for k in range(n_col):
            gain32[k * seqs : (k + 1) * seqs] = jnp.broadcast_to(
                gains[k].astype(jnp.float32), (seqs, feats)
            )

    @pl.when(out_seq)
    def _():
        gather(wo_part, wo_send, wo_recv)

    @pl.when(jnp.logical_not(odd) & (s > 0))
    def _():
        pl.semaphore_signal(go_sem, inc=1, device_id=at(s + 1, r, c), device_id_type=MESH)

    load_keys.wait()
    load_vals.wait()
    score_scale = 1.0 / math.sqrt(hd)

    def summed(region, m, base):
        mixed = pin[region, m, 0].astype(jnp.float32)
        for k in range(1, n_row):
            mixed = mixed + pin[region, m, k].astype(jnp.float32)
        return (base.astype(jnp.float32) + mixed).astype(jnp.bfloat16)

    def hand_over(m, to_section, buffer, same, send_sem, recv_sem):
        @pl.when(same)
        def _():
            pltpu.make_async_remote_copy(
                src_ref=state.at[m],
                dst_ref=buffer.at[m],
                send_sem=send_sem.at[m],
                recv_sem=recv_sem.at[m],
                device_id=at(to_section, r, c),
                device_id_type=MESH,
            ).start()

        @pl.when(jnp.logical_not(same))
        def _():
            for j in [*far_first(n_col), 0]:
                to = lax.rem(c + j, n_col)
                pltpu.make_async_remote_copy(
                    src_ref=state.at[m, to],
                    dst_ref=buffer.at[m, c],
                    send_sem=send_sem.at[m],
                    recv_sem=recv_sem.at[m],
                    device_id=at(to_section, r, to),
                    device_id_type=MESH,
                ).start()

    def take_state(m):
        @pl.when(s == 0)
        def _():
            rows[m] = hidden_ref[m]

        @pl.when(s > 0)
        def _():
            pltpu.make_async_copy(prev.at[m], prev.at[m], prev_recv.at[m]).wait()
            base = rows_of(prev, m, n_blocks)
            pltpu.make_async_copy(pin.at[0, m], pin.at[0, m], po_recv.at[0, m]).wait()
            rows[m] = summed(0, m, base)

        return rows[m]

    def pass_on(m):
        value = rows[m]
        for k in range(n_blocks):
            state[m, k] = value[k * seqs : (k + 1) * seqs]

        @pl.when(s < last)
        def _():
            hand_over(m, s + 1, prev, in_seq == out_seq, prev_send, prev_recv)

        @pl.when(s > 0)
        def _():
            hand_over(m, s - 1, given, in_feat, out_send, out_recv)

        @pl.when((s == last) & in_seq)
        def _():
            given[m, c] = state[m, c]
            for j in far_first(n_col):
                to = lax.rem(c + j, n_col)
                pltpu.make_async_remote_copy(
                    src_ref=state.at[m, to],
                    dst_ref=given.at[m, c],
                    send_sem=prev_send.at[m],
                    recv_sem=out_recv.at[m],
                    device_id=at(s, r, to),
                    device_id_type=MESH,
                ).start()

    def scale(value):
        h_float = value.astype(jnp.float32)
        return h_float * h_float, (h_float * gain32[...]).astype(jnp.bfloat16)

    def project_features(m, carry):
        value = take_state(m)
        squares, scaled = scale(value)
        own_rows = pl.ds(pl.multiple_of(c * feats, feats), feats)
        partial = jnp.dot(scaled, wq[own_rows, :], preferred_element_type=jnp.float32)
        squares = jnp.sum(squares, axis=1, keepdims=True)
        squares = jnp.broadcast_to(squares, (batch, hd))
        for k in range(n_col):
            rs_out[m, k, :, 0:width] = partial[k * seqs : (k + 1) * seqs]
            rs_out[m, k, :, width : width + hd] = squares[k * seqs : (k + 1) * seqs]
        for j in far_first(n_col):
            to = lax.rem(c + j, n_col)
            pltpu.make_async_remote_copy(
                src_ref=rs_out.at[m, to],
                dst_ref=rs_in.at[m, j - 1],
                send_sem=rs_send.at[m],
                recv_sem=rs_recv.at[m],
                device_id=at(s, r, to),
                device_id_type=MESH,
            ).start()
        pass_on(m)
        return carry

    @pl.when(in_feat)
    def _():
        lax.fori_loop(0, micro, project_features, 0)

    region = jnp.where(s == last, 1, 0)
    target = jnp.where(s == last, last, s + 1)

    def send_rows(m):
        def send(j):
            pltpu.make_async_remote_copy(
                src_ref=po.at[m],
                dst_ref=pin.at[region, m, r],
                send_sem=po_send.at[m],
                recv_sem=po_recv.at[region, m],
                device_id=at(target, lax.rem(r + j, n_row), c),
                device_id_type=MESH,
            ).start()

        for j in far_first(n_row):
            send(j)

        @pl.when(s < last)
        def _():
            send(0)

    def attend(m):
        factor = lax.rsqrt(total[:, width : width + hd] / D + 1e-05)
        heads = [total[:, h * hd : (h + 1) * hd] * factor for h in range(per_group + 2)]
        cos = cos8[m]
        sin = sin8[m]

        def rotate(x):
            return (x * cos + pltpu.roll(x, hd // 2, 1) * sin).astype(jnp.bfloat16)

        queries = rotate(jnp.concatenate(heads[:per_group], axis=0))
        new_key = rotate(jnp.concatenate([heads[per_group]] * per_group, axis=0))
        new_value = jnp.concatenate([heads[per_group + 1]] * per_group, axis=0)
        new_value = new_value.astype(jnp.bfloat16).astype(jnp.float32)
        which = lax.rem(row8, seqs)
        scores = None
        for b in range(seqs):
            mine = lax.dot_general(
                queries,
                keys[m, b],
                (((1,), (1,)), ((), ())),
                preferred_element_type=jnp.float32,
            )
            scores = mine if b == 0 else jnp.where(which == b, mine, scores)
        scores = scores * score_scale
        own = queries.astype(jnp.float32) * new_key.astype(jnp.float32)
        own = jnp.sum(own, axis=1, keepdims=True) * score_scale
        scores = jnp.where(lane < lengths_of(m), scores, -jnp.inf)
        top = jnp.maximum(jnp.max(scores, axis=1, keepdims=True), own)
        cache_exp = jnp.exp(scores - top)
        own_exp = jnp.exp(own - top)
        denom = jnp.sum(cache_exp, axis=1, keepdims=True) + own_exp
        weight = (cache_exp / denom).astype(jnp.bfloat16)
        own_weight = (own_exp / denom).astype(jnp.bfloat16).astype(jnp.float32)
        result = None
        for b in range(seqs):
            mine = jnp.dot(weight, vals[m, b], preferred_element_type=jnp.float32)
            result = mine if b == 0 else jnp.where(which == b, mine, result)
        return (result + own_weight * new_value).astype(jnp.bfloat16)

    def middle(m, carry):
        @pl.when(in_feat)
        def _():
            pltpu.make_async_copy(rs_in.at[m], rs_in.at[m], rs_recv.at[m]).wait()
            whole = rs_out[m, c]
            for j in range(n_col - 1):
                whole = whole + rs_in[m, j]
            total[...] = whole

        @pl.when(in_seq)
        def _():
            value = take_state(m)
            squares, scaled = scale(value)
            across = jnp.concatenate(
                [scaled[k * seqs : (k + 1) * seqs] for k in range(n_blocks)], axis=1
            )
            total[:, 0:width] = jnp.dot(across, wq[...], preferred_element_type=jnp.float32)
            both = squares[0:seqs]
            for k in range(1, n_blocks):
                both = both + squares[k * seqs : (k + 1) * seqs]
            both = jnp.sum(both, axis=1, keepdims=True)
            total[:, width : width + hd] = jnp.broadcast_to(both, (seqs, hd))

        result = attend(m)

        @pl.when(out_feat)
        def _():
            for h in range(per_group):
                att[m, c, :, h * hd : (h + 1) * hd] = result[h * seqs : (h + 1) * seqs]
            for j in far_first(n_col):
                pltpu.make_async_remote_copy(
                    src_ref=att.at[m, c],
                    dst_ref=att.at[m, c],
                    send_sem=att_send.at[m],
                    recv_sem=att_recv.at[m],
                    device_id=at(s, r, lax.rem(c + j, n_col)),
                    device_id_type=MESH,
                ).start()

        @pl.when(out_seq)
        def _():
            flat = jnp.concatenate(
                [result[h * seqs : (h + 1) * seqs] for h in range(per_group)], axis=1
            )
            for k in range(n_blocks):
                mixed = jnp.dot(flat, wo[k], preferred_element_type=jnp.float32)
                po[m, k * seqs : (k + 1) * seqs] = mixed.astype(jnp.bfloat16)
            send_rows(m)

        @pl.when(in_seq)
        def _():
            pass_on(m)

        return carry

    lax.fori_loop(0, micro, middle, 0)

    def mix_features(m, carry):
        others = att.at[m, pl.ds(0, n_col - 1)]
        pltpu.make_async_copy(others, others, att_recv.at[m]).wait()
        mixed = jnp.dot(rows_of(att, m, n_col), wo[c], preferred_element_type=jnp.float32)
        mixed = mixed.astype(jnp.bfloat16)
        po[m] = mixed

        @pl.when(s == last)
        def _():
            pin[1, m, r] = mixed

        send_rows(m)
        pltpu.make_async_copy(others, others, att_send.at[m]).wait()
        return carry

    @pl.when(out_feat)
    def _():
        lax.fori_loop(0, micro, mix_features, 0)

    def finish(m, carry):
        @pl.when(s == last)
        def _():
            others = pin.at[1, m, pl.ds(0, n_row - 1)]
            pltpu.make_async_copy(others, others, po_recv.at[1, m]).wait()
            if last - 1 in BY_SEQUENCE:
                blocks = given.at[m, pl.ds(0, n_col - 1)]
                pltpu.make_async_copy(blocks, blocks, out_recv.at[m]).wait()
                pltpu.make_async_copy(blocks, blocks, prev_send.at[m]).wait()
                base = rows_of(given, m, n_blocks)
            else:
                base = rows[m]
            out_ref[m] = summed(1, m, base)
            pltpu.make_async_copy(others, others, po_send.at[m]).wait()

        @pl.when(s < last)
        def _():
            pltpu.make_async_copy(given.at[m], given.at[m], out_recv.at[m]).wait()
            out_ref[m] = rows_of(given, m, n_blocks)
            pltpu.make_async_copy(state.at[m], state.at[m], prev_send.at[m]).wait()
            pltpu.make_async_copy(pin.at[0, m], pin.at[0, m], po_send.at[m]).wait()

        @pl.when(s > 0)
        def _():
            pltpu.make_async_copy(state.at[m], state.at[m], out_send.at[m]).wait()

        @pl.when(in_feat)
        def _():
            pltpu.make_async_copy(rs_in.at[m], rs_in.at[m], rs_send.at[m]).wait()

        return carry

    lax.fori_loop(0, micro, finish, 0)


def solution(mesh):
    n_sec, n_row, n_col = mesh.shape["section"], mesh.shape["row"], mesh.shape["col"]

    def shards(hidden, norm_gain, w_qkv, w_out, cache_keys, cache_values, cache_lengths):
        micro, batch, feats = hidden.shape
        wq = w_qkv[0]
        wo = w_out[0]
        width = wq.shape[1]
        _, _, seqs, length, groups, hd = cache_keys.shape
        keys = cache_keys.reshape(micro, seqs, length, hd)
        vals = cache_values.reshape(micro, seqs, length, hd)
        rows8 = HEADS // KVH * seqs
        bf, f32 = jnp.bfloat16, jnp.float32
        vmem = pl.BlockSpec(memory_space=pltpu.VMEM)
        hbm = pl.BlockSpec(memory_space=pl.ANY)
        sem = pltpu.SemaphoreType.DMA
        out = pl.pallas_call(
            functools.partial(kernel, (n_sec, n_row, n_col)),
            out_shape=jax.ShapeDtypeStruct((micro, batch, feats), bf),
            in_specs=[pl.BlockSpec(memory_space=pltpu.SMEM), vmem, vmem, hbm, hbm, hbm, hbm],
            out_specs=vmem,
            scratch_shapes=[
                pltpu.VMEM((n_col * feats, width), bf),
                pltpu.VMEM((n_col, *wo.shape), bf),
                pltpu.VMEM(keys.shape, bf),
                pltpu.VMEM(vals.shape, bf),
                pltpu.VMEM((micro, rows8, hd), f32),
                pltpu.VMEM((micro, rows8, hd), f32),
                pltpu.VMEM((n_col, 1, feats), bf),
                pltpu.VMEM((batch, feats), f32),
                pltpu.VMEM((micro, batch, feats), bf),
                pltpu.VMEM((micro, n_col, seqs, feats), bf),
                pltpu.VMEM((micro, n_col, seqs, feats), bf),
                pltpu.VMEM((micro, n_col, seqs, feats), bf),
                pltpu.VMEM((2, micro, n_row, batch, feats), bf),
                pltpu.VMEM((micro, n_col, seqs, width + hd), f32),
                pltpu.VMEM((micro, n_col - 1, seqs, width + hd), f32),
                pltpu.VMEM((seqs, width + hd), f32),
                pltpu.VMEM((micro, n_col, seqs, wo.shape[0]), bf),
                pltpu.VMEM((micro, batch, feats), bf),
                sem((4,)),
                sem,
                sem((2, n_col // 2, CHUNKS)),
                sem,
                sem((2, n_col // 2, CHUNKS)),
                sem,
                sem,
                pltpu.SemaphoreType.REGULAR,
                sem((micro,)),
                sem((micro,)),
                sem((micro,)),
                sem((micro,)),
                sem((micro,)),
                sem((2, micro)),
                sem((micro,)),
                sem((micro,)),
                sem((micro,)),
                sem((micro,)),
            ],
            compiler_params=pltpu.CompilerParams(
                collective_id=0, has_side_effects=True, vmem_limit_bytes=48 << 20
            ),
        )(cache_lengths.reshape(-1), hidden, norm_gain, wq, wo, keys, vals)
        return out[None]

    return jax.shard_map(
        shards,
        mesh=mesh,
        in_specs=(
            P(None, None, "col"),
            P("section", "col"),
            P("section", "col", "row"),
            P("section", "row", "col"),
            P("section", None, "col", None, "row", None),
            P("section", None, "col", None, "row", None),
            P(None, "col"),
        ),
        out_specs=P("section", None, None, "col"),
        check_vma=False,
    )
```

time: 205 us -> 183 us (0.89)
  Pallas kernels: 202 us -> 176 us
  local copies, waits for them, and re-layouts: 2.84 us -> 6.76 us
    pallas_call x1, Pallas kernels: 202 us -> 176 us  [shards(): pl.pallas_call(functools.partial(kernel, (n_sec, n_row, n_col)), out_shap...]
    unnamed x4 -> x16, local copies, waits for them, and re-layouts: 2.24 us -> 6.68 us
where the time goes in v2:
time: 183 us
  Pallas kernels  176 us (96%)
  local copies, waits for them, and re-layouts  6.76 us (4%)
    pallas_call x1, Pallas kernels, shards(): pl.pallas_call(functools.partial(kernel, (n_sec, n_row, n_col)), out_shap...  176 us
    unnamed x16, local copies, waits for them, and re-layouts  6.68 us

profile of v2, /device:TPU:7, one launch (start us, length us, event | category | flops | bytes accessed | tf_op | source)
XLA Modules:
  0.0 183.1 jit_solution(2438493072210872694)
XLA Ops:
  0.0 0.0 copy-start.6
  0.0 0.7 copy-done.6
  0.7 0.1 copy.9
  0.8 0.0 copy-start.5
  0.8 0.1 reshape.9.lens_ref
  0.9 0.6 copy-done.5
  1.5 0.0 copy-start
  1.5 1.0 copy-done
  2.4 0.0 copy-start.1
  2.5 0.9 copy-done.1
  3.4 0.0 copy-start.2
  3.4 0.9 copy-done.2
  4.3 0.0 copy-start.3
  4.4 0.9 copy-done.3
  5.3 0.0 copy-start.4
  5.3 0.8 copy-done.4
  6.1 176.3 %shard_map.73 = bf16[4,32,256]{2,1,0:T(8,128)(2,1)S(1)} custom-call(s32[8]{0:T(128)S(1)} %reshape.9.lens_ref, bf16[4,32,256]{2,1,0:T(8,128)(2,1)S(1)} %copy-done.4, bf16[1,256]{1,0:T(2,128)(2,1)S(1)} %copy-done.5, bf16[256,768]{1,0:T(8,128)(2,1)S(1)} %bitcast.5, bf16[512,256]{1,0:T(8,128)(2,1)S(1)} %bitcast.7, bf16[4,2,128,128]{3,2,1,0:T(8,128)(2,1)S(1)} %bitcast.8, ...), custom_call_target="tpu_custom_call" | custom-call | tf_op jit(solution)/shard_map/pallas_call | solution.py:557
  182.5 0.6 copy.11
Async XLA Ops:
  0.0 0.7 copy-start.6
  0.8 0.7 copy-start.5
  1.5 1.0 copy-start
  2.4 0.9 copy-start.1
  3.4 0.9 copy-start.2
  4.3 0.9 copy-start.3
  5.3 0.8 copy-start.4

commit v3 on v2

--- a/solution.py
+++ b/solution.py
@@ -12,7 +12,7 @@
 HEADS = 32
 KVH = 8
 MESH = pl.DeviceIdType.MESH
-BY_SEQUENCE = (1, 3, 4, 6)
+BY_SEQUENCE = (3, 5, 6)
 CHUNKS = 4
 
 
@@ -38,14 +38,17 @@
 
 def kernel(
     sizes,
-    lens_ref,
-    hidden_ref,
-    gain_ref,
+    lens_hbm,
+    hidden_hbm,
+    gain_hbm,
     wq_hbm,
     wo_hbm,
     keys_hbm,
     vals_hbm,
     out_ref,
+    lens_ref,
+    hidden_ref,
+    gain_ref,
     wq,
     wo,
     keys,
@@ -108,6 +111,12 @@
     load_wo = pltpu.make_async_copy(wo_hbm, wo.at[c], load_sem.at[1])
     load_keys = pltpu.make_async_copy(keys_hbm, keys, load_sem.at[2])
     load_vals = pltpu.make_async_copy(vals_hbm, vals, load_sem.at[3])
+    load_lens = pltpu.make_async_copy(lens_hbm, lens_ref, load_sem.at[4])
+    load_gain = pltpu.make_async_copy(gain_hbm, gain_ref, load_sem.at[5])
+    load_hidden = pltpu.make_async_copy(hidden_hbm, hidden_ref, load_sem.at[6])
+    load_lens.start()
+    load_gain.start()
+    load_hidden.start()
     load_wq.start()
     load_wo.start()
     load_keys.start()
@@ -140,6 +149,10 @@
         for j in range(1, n_row):
             greet(at(s, lax.rem(r + j, n_row), c))
 
+    load_lens.wait()
+    load_gain.wait()
+    load_hidden.wait()
+
     lane = lax.broadcasted_iota(jnp.int32, (rows8, hd), 1)
     row8 = lax.broadcasted_iota(jnp.int32, (rows8, hd), 0)
     half = lax.rem(lane, hd // 2).astype(jnp.float32)
@@ -147,9 +160,9 @@
     sign = jnp.where(lane < hd // 2, -1.0, 1.0)
 
     def lengths_of(m):
-        value = jnp.full((rows8, hd), lens_ref[m * seqs], jnp.int32)
+        value = jnp.full((rows8, hd), lens_ref[0, m], jnp.int32)
         for b in range(1, seqs):
-            value = jnp.where(lax.rem(row8, seqs) == b, lens_ref[m * seqs + b], value)
+            value = jnp.where(lax.rem(row8, seqs) == b, lens_ref[b, m], value)
         return value
 
     for m in range(micro):
@@ -189,24 +202,27 @@
             copy(0, 0, c, piece, right).start()
             copy(1, 0, c, piece, left).start()
 
-        rightward, leftward = n_col // 2, n_col - 1 - n_col // 2
+        steps = n_col // 2
 
         def forward(step, carry):
             for piece in range(CHUNKS):
                 arrived(0, step - 1, piece)
-                copy(0, step, lax.rem(c + n_col - step, n_col), piece, right).start()
-
-                @pl.when(step < leftward)
+
+                @pl.when((step < steps - 1) | (piece < CHUNKS // 2))
                 def _():
-                    arrived(1, step - 1, piece)
+                    copy(0, step, lax.rem(c + n_col - step, n_col), piece, right).start()
+
+                arrived(1, step - 1, piece)
+
+                @pl.when((step < steps - 1) | (piece >= CHUNKS // 2))
+                def _():
                     copy(1, step, lax.rem(c + step, n_col), piece, left).start()
 
             return carry
 
-        lax.fori_loop(1, rightward, forward, 0)
+        lax.fori_loop(1, steps, forward, 0)
         for piece in range(CHUNKS):
-            arrived(0, rightward - 1, piece)
-            arrived(1, leftward - 1, piece)
+            arrived(0 if piece < CHUNKS // 2 else 1, steps - 1, piece)
 
         def sent(k, carry):
             for piece in range(CHUNKS):
@@ -340,7 +356,7 @@
         h_float = value.astype(jnp.float32)
         return h_float * h_float, (h_float * gain32[...]).astype(jnp.bfloat16)
 
-    def project_features(m, carry):
+    def project_features(m):
         value = take_state(m)
         squares, scaled = scale(value)
         own_rows = pl.ds(pl.multiple_of(c * feats, feats), feats)
@@ -361,11 +377,6 @@
                 device_id_type=MESH,
             ).start()
         pass_on(m)
-        return carry
-
-    @pl.when(in_feat)
-    def _():
-        lax.fori_loop(0, micro, project_features, 0)
 
     region = jnp.where(s == last, 1, 0)
     target = jnp.where(s == last, last, s + 1)
@@ -427,7 +438,7 @@
             result = mine if b == 0 else jnp.where(which == b, mine, result)
         return (result + own_weight * new_value).astype(jnp.bfloat16)
 
-    def middle(m, carry):
+    def middle(m):
         @pl.when(in_feat)
         def _():
             pltpu.make_async_copy(rs_in.at[m], rs_in.at[m], rs_recv.at[m]).wait()
@@ -480,11 +491,8 @@
         def _():
             pass_on(m)
 
-        return carry
-
-    lax.fori_loop(0, micro, middle, 0)
-
-    def mix_features(m, carry):
+
+    def mix_features(m):
         others = att.at[m, pl.ds(0, n_col - 1)]
         pltpu.make_async_copy(others, others, att_recv.at[m]).wait()
         mixed = jnp.dot(rows_of(att, m, n_col), wo[c], preferred_element_type=jnp.float32)
@@ -496,12 +504,23 @@
             pin[1, m, r] = mixed
 
         send_rows(m)
-        pltpu.make_async_copy(others, others, att_send.at[m]).wait()
+
+    def step(t, carry):
+        @pl.when(in_feat & (t < micro))
+        def _():
+            project_features(t)
+
+        @pl.when((t >= 2) & (t < micro + 2))
+        def _():
+            middle(t - 2)
+
+        @pl.when(out_feat & (t >= 4))
+        def _():
+            mix_features(t - 4)
+
         return carry
 
-    @pl.when(out_feat)
-    def _():
-        lax.fori_loop(0, micro, mix_features, 0)
+    lax.fori_loop(0, micro + 4, step, 0)
 
     def finish(m, carry):
         @pl.when(s == last)
@@ -533,6 +552,11 @@
         def _():
             pltpu.make_async_copy(rs_in.at[m], rs_in.at[m], rs_send.at[m]).wait()
 
+        @pl.when(out_feat)
+        def _():
+            others = att.at[m, pl.ds(0, n_col - 1)]
+            pltpu.make_async_copy(others, others, att_send.at[m]).wait()
+
         return carry
 
     lax.fori_loop(0, micro, finish, 0)
@@ -552,14 +576,17 @@
         rows8 = HEADS // KVH * seqs
         bf, f32 = jnp.bfloat16, jnp.float32
         vmem = pl.BlockSpec(memory_space=pltpu.VMEM)
-        hbm = pl.BlockSpec(memory_space=pl.ANY)
+        hbm = pl.BlockSpec(memory_space=pltpu.HBM)
         sem = pltpu.SemaphoreType.DMA
         out = pl.pallas_call(
             functools.partial(kernel, (n_sec, n_row, n_col)),
             out_shape=jax.ShapeDtypeStruct((micro, batch, feats), bf),
-            in_specs=[pl.BlockSpec(memory_space=pltpu.SMEM), vmem, vmem, hbm, hbm, hbm, hbm],
+            in_specs=[hbm] * 7,
             out_specs=vmem,
             scratch_shapes=[
+                pltpu.SMEM((seqs, micro), jnp.int32),
+                pltpu.VMEM(hidden.shape, bf),
+                pltpu.VMEM(norm_gain.shape, bf),
                 pltpu.VMEM((n_col * feats, width), bf),
                 pltpu.VMEM((n_col, *wo.shape), bf),
                 pltpu.VMEM(keys.shape, bf),
@@ -578,7 +605,7 @@
                 pltpu.VMEM((seqs, width + hd), f32),
                 pltpu.VMEM((micro, n_col, seqs, wo.shape[0]), bf),
                 pltpu.VMEM((micro, batch, feats), bf),
-                sem((4,)),
+                sem((7,)),
                 sem,
                 sem((2, n_col // 2, CHUNKS)),
                 sem,
@@ -598,9 +625,9 @@
                 sem((micro,)),
             ],
             compiler_params=pltpu.CompilerParams(
-                collective_id=0, has_side_effects=True, vmem_limit_bytes=48 << 20
+                collective_id=0, has_side_effects=True, vmem_limit_bytes=67000000
             ),
-        )(cache_lengths.reshape(-1), hidden, norm_gain, wq, wo, keys, vals)
+        )(cache_lengths.T, hidden, norm_gain, wq, wo, keys, vals)
         return out[None]
 
     return jax.shard_map(

time: 183 us -> 152 us (0.83)
  Pallas kernels: 176 us -> 151 us
  local copies, waits for them, and re-layouts: 6.76 us -> 1.47 us
    pallas_call x1, Pallas kernels: 176 us -> 151 us  [shards(): pl.pallas_call(functools.partial(kernel, (n_sec, n_row, n_col)), out_shap...]
    unnamed x16 -> x1, local copies, waits for them, and re-layouts: 6.68 us -> 1.47 us
where the time goes in v3:
time: 152 us
  Pallas kernels  151 us (99%)
    pallas_call x1, Pallas kernels, shards(): pl.pallas_call(functools.partial(kernel, (n_sec, n_row, n_col)), out_shap...  151 us

profile of v3, /device:TPU:7, one launch (start us, length us, event | category | flops | bytes accessed | tf_op | source)
XLA Modules:
  0.0 152.2 jit_solution(17327692442391305735)
XLA Ops:
  0.0 150.7 %shard_map.73 = bf16[4,32,256]{2,1,0:T(8,128)(2,1)} custom-call(s32[2,4]{1,0:T(2,128)} %bitcast.11, bf16[4,32,256]{2,1,0:T(8,128)(2,1)} %hidden_hbm.1, bf16[1,256]{1,0:T(2,128)(2,1)} %gain_hbm.1, bf16[256,768]{1,0:T(8,128)(2,1)} %bitcast.6, bf16[512,256]{1,0:T(8,128)(2,1)} %bitcast.7, bf16[4,2,128,128]{3,2,1,0:T(8,128)(2,1)} %bitcast.8, ...), custom_call_target="tpu_custom_call" | custom-call | tf_op jit(solution)/shard_map/pallas_call | solution.py:581
  150.7 1.5 copy.9

commit v4 on v3

--- a/solution.py
+++ b/solution.py
@@ -281,9 +281,9 @@
     score_scale = 1.0 / math.sqrt(hd)
 
     def summed(region, m, base):
-        mixed = pin[region, m, 0].astype(jnp.float32)
+        mixed = pin[region, m, 0]
         for k in range(1, n_row):
-            mixed = mixed + pin[region, m, k].astype(jnp.float32)
+            mixed = mixed + pin[region, m, k]
         return (base.astype(jnp.float32) + mixed).astype(jnp.bfloat16)
 
     def hand_over(m, to_section, buffer, same, send_sem, recv_sem):
@@ -484,7 +484,7 @@
             )
             for k in range(n_blocks):
                 mixed = jnp.dot(flat, wo[k], preferred_element_type=jnp.float32)
-                po[m, k * seqs : (k + 1) * seqs] = mixed.astype(jnp.bfloat16)
+                po[m, k * seqs : (k + 1) * seqs] = mixed
             send_rows(m)
 
         @pl.when(in_seq)
@@ -496,7 +496,6 @@
         others = att.at[m, pl.ds(0, n_col - 1)]
         pltpu.make_async_copy(others, others, att_recv.at[m]).wait()
         mixed = jnp.dot(rows_of(att, m, n_col), wo[c], preferred_element_type=jnp.float32)
-        mixed = mixed.astype(jnp.bfloat16)
         po[m] = mixed
 
         @pl.when(s == last)
@@ -599,12 +598,12 @@
                 pltpu.VMEM((micro, n_col, seqs, feats), bf),
                 pltpu.VMEM((micro, n_col, seqs, feats), bf),
                 pltpu.VMEM((micro, n_col, seqs, feats), bf),
-                pltpu.VMEM((2, micro, n_row, batch, feats), bf),
+                pltpu.VMEM((2, micro, n_row, batch, feats), f32),
                 pltpu.VMEM((micro, n_col, seqs, width + hd), f32),
                 pltpu.VMEM((micro, n_col - 1, seqs, width + hd), f32),
                 pltpu.VMEM((seqs, width + hd), f32),
                 pltpu.VMEM((micro, n_col, seqs, wo.shape[0]), bf),
-                pltpu.VMEM((micro, batch, feats), bf),
+                pltpu.VMEM((micro, batch, feats), f32),
                 sem((7,)),
                 sem,
                 sem((2, n_col // 2, CHUNKS)),

time: 152 us -> 164 us (1.079)
  Pallas kernels: 151 us -> 162 us
    pallas_call x1, Pallas kernels: 151 us -> 162 us  [shards(): pl.pallas_call(functools.partial(kernel, (n_sec, n_row, n_col)), out_shap...]
where the time goes in v4:
time: 164 us
  Pallas kernels  162 us (99%)
    pallas_call x1, Pallas kernels, shards(): pl.pallas_call(functools.partial(kernel, (n_sec, n_row, n_col)), out_shap...  162 us

profile of v4, /device:TPU:7, one launch (start us, length us, event | category | flops | bytes accessed | tf_op | source)
XLA Modules:
  0.0 163.6 jit_solution(12163056683513449849)
XLA Ops:
  0.0 162.2 %shard_map.73 = bf16[4,32,256]{2,1,0:T(8,128)(2,1)} custom-call(s32[2,4]{1,0:T(2,128)} %bitcast.11, bf16[4,32,256]{2,1,0:T(8,128)(2,1)} %hidden_hbm.1, bf16[1,256]{1,0:T(2,128)(2,1)} %gain_hbm.1, bf16[256,768]{1,0:T(8,128)(2,1)} %bitcast.6, bf16[512,256]{1,0:T(8,128)(2,1)} %bitcast.7, bf16[4,2,128,128]{3,2,1,0:T(8,128)(2,1)} %bitcast.8, ...), custom_call_target="tpu_custom_call" | custom-call | tf_op jit(solution)/shard_map/pallas_call | solution.py:580
  162.2 1.5 copy.9

commit v5 on v3

--- a/solution.py
+++ b/solution.py
@@ -101,6 +101,8 @@
     out_feat = jnp.logical_not(out_seq)
     in_seq = one_of(s, [b + 1 for b in BY_SEQUENCE])
     in_feat = jnp.logical_not(in_seq)
+    spread_out = in_seq | out_seq
+    spread_in = in_seq | one_of(s, [b + 2 for b in BY_SEQUENCE])
     right, left = lax.rem(c + 1, n_col), lax.rem(c + n_col - 1, n_col)
 
     def at(sec, row, col):
@@ -134,6 +136,9 @@
     def _():
         for j in range(n_row):
             greet(at(s + 1, lax.rem(r + j, n_row), c))
+
+    @pl.when((s < last) & spread_out)
+    def _():
         for j in range(1, n_col):
             greet(at(s + 1, r, lax.rem(c + j, n_col)))
 
@@ -141,6 +146,9 @@
     def _():
         for j in range(n_row):
             greet(at(s - 1, lax.rem(r + j, n_row), c))
+
+    @pl.when((s > 0) & spread_in)
+    def _():
         for j in range(1, n_col):
             greet(at(s - 1, r, lax.rem(c + j, n_col)))
 
@@ -174,13 +182,14 @@
 
     load_wq.wait()
     load_wo.wait()
-    across = n_row + n_col - 1
     pl.semaphore_wait(
         barrier,
         n_col
         - 1
-        + jnp.where(s < last, across, 0)
-        + jnp.where(s > 0, across, 0)
+        + jnp.where(s < last, n_row, 0)
+        + jnp.where((s < last) & spread_out, n_col - 1, 0)
+        + jnp.where(s > 0, n_row, 0)
+        + jnp.where((s > 0) & spread_in, n_col - 1, 0)
         + jnp.where(s == last, n_row - 1, 0),
     )
 

time: 152 us -> 153 us (level)
  no operation moved by 1% of the time
where the time goes in v5:
time: 153 us; the launch traced here: 152 us
  Pallas kernels  151 us (99%)
    pallas_call x1, Pallas kernels, shards(): pl.pallas_call(functools.partial(kernel, (n_sec, n_row, n_col)), out_shap...  151 us

profile of v5, /device:TPU:7, one launch (start us, length us, event | category | flops | bytes accessed | tf_op | source)
XLA Modules:
  0.0 152.4 jit_solution(9150871910854300291)
XLA Ops:
  0.0 150.9 %shard_map.73 = bf16[4,32,256]{2,1,0:T(8,128)(2,1)} custom-call(s32[2,4]{1,0:T(2,128)} %bitcast.11, bf16[4,32,256]{2,1,0:T(8,128)(2,1)} %hidden_hbm.1, bf16[1,256]{1,0:T(2,128)(2,1)} %gain_hbm.1, bf16[256,768]{1,0:T(8,128)(2,1)} %bitcast.6, bf16[512,256]{1,0:T(8,128)(2,1)} %bitcast.7, bf16[4,2,128,128]{3,2,1,0:T(8,128)(2,1)} %bitcast.8, ...), custom_call_target="tpu_custom_call" | custom-call | tf_op jit(solution)/shard_map/pallas_call | solution.py:590
  151.0 1.5 copy.9
